TPU v7x, 768 devices: a whole 4x8x12 slice. The times are simulated.
768 devices in a mesh: ep: 48 (over y_hi, z), tp: 16 (over x, y_lo, core).
Axes of the slice: x: 4, y: 8 (y_hi: 4, y_lo: 2; y = y_hi * 2 + y_lo), z: 12, core: 2. Of those that a mesh axis runs over, the one named last changes fastest.
Arguments:
- tokens: bfloat16 [1536, 6144], P('ep', 'tp'), may hold values from -6 to 6
- expert_ids: int32 [1536, 8], P('ep'), may hold values from 0 to 47, all different within a row; in each aligned block of 32 rows (0 to 31, 32 to 63, ...) at most 10 rows name the same one
- gate_scores: float32 [1536, 8], P('ep'), may hold values from 0.05 to 0.6
- routed_gate: bfloat16 [48, 6144, 2048], P('ep', None, 'tp'), may hold values from -0.078125 to 0.078125
- routed_up: bfloat16 [48, 6144, 2048], P('ep', None, 'tp'), may hold values from -0.078125 to 0.078125
- routed_down: bfloat16 [48, 2048, 6144], P('ep', 'tp'), may hold values from -0.1875 to 0.1875
- shared_gate: bfloat16 [6144, 2048], P(None, 'tp'), may hold values from -0.078125 to 0.078125
- shared_up: bfloat16 [6144, 2048], P(None, 'tp'), may hold values from -0.078125 to 0.078125
- shared_down: bfloat16 [2048, 6144], P('tp'), may hold values from -0.1875 to 0.1875
Outputs:
- moe_out: bfloat16 [1536, 6144], P('ep', 'tp')
Inputs may be any that keep to these rules, and one draw needn't show every extreme that they name: `expert_ids`: each row names 8 different experts. Among the 32 rows of one aligned block no expert is named more than 10 times, and in some block one expert is named exactly 10 times.
All inputs are finite; a program needn't handle non-finite values.
Results may differ from a plain program's by a relative error of at most 0.019.
Values may be sent and summed in bfloat16 or wider, within the bound.
No kernel may reach another device: no remote copies, remote signals or barrier semaphores. Data moves between devices by JAX's collectives and lax.ppermute only.
A program may use at most 128 MiB of HBM per device.

v0:
```python
import jax
import jax.numpy as jnp
from jax import lax
from jax.sharding import PartitionSpec as P


def split_up(shard, dim, length):
    lengths = shard.shape
    tiles = shard.reshape(*lengths[:dim], length, lengths[dim] // length, *lengths[dim + 1 :])
    return jnp.moveaxis(tiles, dim, 0)


def one_scatter(arrays, axis, dims):
    length = lax.axis_size(axis)
    tiles = [split_up(a, dim, length) for a, dim in zip(arrays, dims)]
    lines = jnp.concatenate([b.reshape(length, -1) for b in tiles], axis=1)
    extent = max(16, -(-lines.shape[1] // 1024) * 8)
    lines = jnp.pad(lines, ((0, 0), (0, extent * 128 - lines.shape[1]))).reshape(-1, 128)
    vector, at, outs = (lax.psum_scatter(lines, axis, tiled=True).reshape(-1), 0, [])
    for b in tiles:
        part = b[0]
        outs.append(vector[at : at + part.size].reshape(part.shape))
        at += part.size
    return tuple(outs)


def routing(expert_ids, gate_scores, experts, capacity):
    row_count, top_count = expert_ids.shape
    entries = expert_ids.reshape(-1)
    onehot = (entries[:, None] == jnp.arange(experts, dtype=jnp.int32)[None, :]).astype(jnp.int32)
    before = jnp.cumsum(onehot, axis=0, dtype=jnp.int32) - onehot
    slot_rank = jnp.sum(before * onehot, axis=1)
    position = entries * capacity + slot_rank
    places = jnp.arange(experts * capacity, dtype=jnp.int32)[:, None] == position[None, :]
    places = places.reshape(experts * capacity, row_count, top_count).astype(jnp.float32)
    select = jnp.sum(places, axis=2).astype(jnp.bfloat16)
    combine_weights = jnp.sum(places * gate_scores[None, :, :], axis=2)
    return (select, combine_weights)


def full_pass(whole_rows, w_gate, w_up, w_down):
    gate_sum = jnp.dot(whole_rows, w_gate, preferred_element_type=jnp.float32)
    up_sum = jnp.dot(whole_rows, w_up, preferred_element_type=jnp.float32)
    hidden = (jax.nn.silu(gate_sum) * up_sum).astype(jnp.bfloat16)
    return jnp.dot(hidden, w_down, preferred_element_type=jnp.float32).astype(jnp.bfloat16)


def local(
    tokens,
    expert_ids,
    gate_scores,
    routed_gate,
    routed_up,
    routed_down,
    shared_gate,
    shared_up,
    shared_down,
):
    experts = routed_gate.shape[0] * lax.axis_size("ep")
    row_count, top_count = expert_ids.shape
    capacity = min(row_count, row_count * top_count * 15 // (8 * experts))
    select, combine_weights = routing(expert_ids, gate_scores, experts, capacity)
    width_local = tokens.shape[1]
    buckets = jnp.dot(select, tokens, preferred_element_type=jnp.float32).astype(jnp.bfloat16)
    buckets = buckets.reshape(experts, capacity, width_local)
    w_gate = routed_gate[0]
    w_up = routed_up[0]
    w_down = routed_down[0]
    received = lax.all_to_all(buckets, "ep", split_axis=0, concat_axis=0, tiled=True)
    routed_rows, shared_rows = (
        lax.all_gather(received, "tp", axis=2, tiled=True),
        lax.all_gather(tokens, "tp", axis=1, tiled=True),
    )
    routed_partial = full_pass(routed_rows, w_gate, w_up, w_down)
    shared_partial = full_pass(shared_rows, shared_gate, shared_up, shared_down)
    routed_sum, shared_out = tuple(
        (
            part.astype(jnp.float32)
            for part in one_scatter((routed_partial, shared_partial), "tp", (2, 1))
        )
    )
    returned = lax.all_to_all(
        routed_sum.astype(jnp.bfloat16), "ep", split_axis=0, concat_axis=0, tiled=True
    )
    flat_returned = returned.reshape(experts * capacity, width_local).astype(jnp.float32)
    routed = jnp.einsum(
        "pt,pd->td", combine_weights, flat_returned, precision=lax.Precision.HIGHEST
    )
    return (routed + shared_out).astype(jnp.bfloat16)


def solution(mesh):
    placed = (
        P("ep", "tp"),
        P("ep", None),
        P("ep", None),
        P("ep", None, "tp"),
        P("ep", None, "tp"),
        P("ep", "tp", None),
        P(None, "tp"),
        P(None, "tp"),
        P("tp", None),
    )
    return jax.shard_map(
        local, mesh=mesh, in_specs=placed, out_specs=P("ep", "tp"), check_vma=False
    )
```

profile of v0, /device:TPU:1, one launch (start us, length us, event | category | flops | bytes accessed | tf_op | source)
XLA Modules:
  0.0 298.5 jit_solution(17703284448840232643)
XLA Ops:
  6.5 0.0 copy-start
  6.5 0.0 all-gather.2.cloned.1.call-start
  6.5 0.9 copy.29
  7.4 0.1 eq.44
  7.5 0.1 eq.40
  7.6 0.6 reduce-window.6
  8.2 0.2 slice_reduce_fusion
  8.4 0.1 fusion.23
  8.6 0.1 reduce_sum.30
  8.7 0.8 copy.33
  9.4 1.0 select_reduce_fusion
  10.4 1.0 convolution_convert_fusion.2
  11.5 0.1 reshape.69
  11.6 48.1 %all_to_all.10 = bf16[48,10,384]{2,1,0:T(8,128)(2,1)S(1)} all-to-all(bf16[48,10,384]{2,1,0:T(8,128)(2,1)S(1)} %reshape.69), channel_id=1, replica_groups=mesh['ep'=48,'tp'=16] {'ep'}, dimensions={0} | all-to-all | bytes 737280 | tf_op jit(solution)/shard_map/all_to_all | solution.py:69
  59.7 0.0 copy-start.2
  59.7 0.8 copy.34
  60.5 0.0 all-gather.2.cloned.1.call-update
  60.6 0.0 reduce-scatter.2.cloned.1.call-start
  60.6 25.6 %all_gather.7 = bf16[32,6144]{1,0:T(8,128)(2,1)S(1)} all-gather(bf16[32,384]{1,0:T(8,128)(2,1)} %param.9), channel_id=1, replica_groups=mesh['ep'=48,'tp'=16] {'tp'}, dimensions={1}, use_global_device_ids=true | all-gather | bytes 417792 | tf_op jit(solution)/shard_map/all_gather | solution.py:72
  86.2 0.0 copy-done.2
  86.2 0.4 fusion.34
  86.5 2.6 convolution_convert_fusion.1
  89.2 0.1 copy.40
  89.3 0.0 copy-start.1
  89.4 16.5 %all-gather.2.cloned.1.call-done = bf16[48,10,6144]{2,0,1:T(8,128)(2,1)} async-done(((bf16[48,10,384]{2,0,1:T(8,128)(2,1)}), bf16[48,10,6144]{2,0,1:T(8,128)(2,1)}) %all-gather.2.cloned.1.call-update) | async-done | bytes 5898256 | tf_op jit(solution)/shard_map/all_gather | solution.py:71
  105.9 5.5 %fusion.3 = f32[48,10,128]{2,0,1:T(8,128)} fusion(bf16[48,10,6144]{2,0,1:T(8,128)(2,1)} %all-gather.2.cloned.1.call-done, bf16[1,6144,128]{2,1,0:T(8,128)(2,1)} %param.12), kind=kOutput, calls=%fused_computation.7 | convolution fusion | flops 754974720 | bytes 7716864 | tf_op jit(solution)/shard_map/dot_general | solution.py:42
  111.4 0.0 copy-done
  111.4 0.0 copy-done.1
  111.4 11.5 %convolution_convert_fusion = bf16[48,10,6144]{2,0,1:T(8,128)(2,1)} fusion(bf16[1,128,6144]{2,1,0:T(8,128)(2,1)S(1)} %copy-done, bf16[48,10,6144]{2,0,1:T(8,128)(2,1)} %all-gather.2.cloned.1.call-done, bf16[1,6144,128]{2,1,0:T(8,128)(2,1)S(1)} %copy-done.1, f32[48,10,128]{2,0,1:T(8,128)} %fusion.3), kind=kOutput, calls=%fused_computation.1 | convolution fusion | flops 1513267200 | bytes 15187968 | tf_op jit(solution)/shard_map/dot_general | solution.py:45
  122.9 6.7 %copy.39 = bf16[60,8,16,384]{3,2,1,0:T(8,128)(2,1)} copy(bf16[60,8,16,384]{3,1,2,0:T(8,128)(2,1)} %bitcast.65) | data formatting | bytes 11796480
  129.6 10.4 %copy.44 = bf16[48,10,16,384]{3,1,0,2:T(8,128)(2,1)} copy(bf16[48,10,16,384]{3,2,0,1:T(8,128)(2,1)} %bitcast.66) | data formatting | bytes 11796480 | tf_op jit(solution)/shard_map/reshape | solution.py:9
  140.0 11.4 %reshape.71 = bf16[16,184320]{1,0:T(8,128)(2,1)} reshape(bf16[16,48,10,384]{3,2,1,0:T(8,128)(2,1)} %bitcast.64) | data formatting | bytes 11796480 | tf_op jit(solution)/shard_map/reshape | solution.py:16
  151.4 9.0 %pad_maximum_fusion = bf16[16,196608]{1,0:T(8,128)(2,1)} fusion(bf16[16,12288]{1,0:T(8,128)(2,1)S(1)} %bitcast.67, bf16[16,184320]{1,0:T(8,128)(2,1)} %reshape.71), kind=kLoop, calls=%fused_computation.3 | loop fusion | flops 12582912 | bytes 12582912 | tf_op jit(solution)/shard_map/concatenate | solution.py:16
  160.4 6.4 %reshape.74 = bf16[24576,128]{1,0:T(8,128)(2,1)} reshape(bf16[16,196608]{1,0:T(8,128)(2,1)} %pad_maximum_fusion) | data formatting | bytes 12582912 | tf_op jit(solution)/shard_map/reshape | solution.py:18
  166.8 0.0 reduce-scatter.2.cloned.1.call-update
  166.8 83.1 %reduce-scatter.2.cloned.1.call-done = bf16[1536,128]{1,0:T(8,128)(2,1)} async-done(((bf16[24576,128]{1,0:T(8,128)(2,1)}), bf16[1536,128]{1,0:T(8,128)(2,1)}) %reduce-scatter.2.cloned.1.call-update) | async-done | bytes 393232 | tf_op jit(solution)/shard_map/reduce_scatter | solution.py:19
  249.9 1.0 slice.19
  250.9 0.0 copy-start.3
  250.9 1.0 reshape.75
  251.9 14.2 %all-to-all-start.1 = ((bf16[48,10,384]{2,1,0:T(8,128)(2,1)}), bf16[48,10,384]{2,1,0:T(8,128)(2,1)S(1)}, u32[]{:S(2)}, u32[]{:S(2)}) async-start(bf16[48,10,384]{2,1,0:T(8,128)(2,1)} %reshape.75), calls=%async_computation.2 | async-start | bytes 1179648 | tf_op jit(solution)/shard_map/all_to_all | solution.py:82
  266.2 0.7 slice_convert_fusion
  266.9 23.6 %all-to-all-done.1 = bf16[48,10,384]{2,1,0:T(8,128)(2,1)S(1)} async-done(((bf16[48,10,384]{2,1,0:T(8,128)(2,1)}), bf16[48,10,384]{2,1,0:T(8,128)(2,1)S(1)}, u32[]{:S(2)}, u32[]{:S(2)}) %all-to-all-start.1) | async-done | bytes 368672 | tf_op jit(solution)/shard_map/all_to_all | solution.py:82
  290.6 0.1 reshape.76
  290.7 0.0 copy-done.3
  290.7 0.9 fusion.13
  (6 shorter events, 0.1 us)
Async XLA Ops:
  6.5 104.9 %copy-start = (bf16[1,128,6144]{2,1,0:T(8,128)(2,1)S(1)}, bf16[1,128,6144]{2,1,0:T(8,128)(2,1)}, u32[]{:S(2)}) copy-start(bf16[1,128,6144]{2,1,0:T(8,128)(2,1)} %param.14) | copy-start | bytes 4718596
  6.5 99.3 %all-gather.2.cloned.1.call-start = ((), (), s32[]{:S(2)}) async-start(), calls=%async_computation.3 | async-start | bytes 6266880 | tf_op jit(solution)/shard_map/all_gather | solution.py:71
  59.7 26.5 %copy-start.2 = (bf16[6144,128]{1,0:T(8,128)(2,1)S(1)}, bf16[6144,128]{1,0:T(8,128)(2,1)}, u32[]{:S(2)}) copy-start(bf16[6144,128]{1,0:T(8,128)(2,1)} %param.15) | copy-start | bytes 4718596
  60.6 189.3 %reduce-scatter.2.cloned.1.call-start = ((), (), s32[]{:S(2)}) async-start(), calls=%async_computation.4 | async-start | bytes 6684672 | tf_op jit(solution)/shard_map/reduce_scatter | solution.py:19
  89.3 22.1 %copy-start.1 = (bf16[1,6144,128]{2,1,0:T(8,128)(2,1)S(1)}, bf16[1,6144,128]{2,1,0:T(8,128)(2,1)}, u32[]{:S(2)}) copy-start(bf16[1,6144,128]{2,1,0:T(8,128)(2,1)} %param.13) | copy-start | bytes 4718596
  250.9 39.8 %copy-start.3 = (f32[480,32]{0,1:T(8,128)S(1)}, f32[480,32]{0,1:T(8,128)}, u32[]{:S(2)}) copy-start(f32[480,32]{0,1:T(8,128)} %get-tuple-element.5) | copy-start | bytes 184324
  251.9 38.6 %all-to-all-start.1 = ((bf16[48,10,384]{2,1,0:T(8,128)(2,1)}), bf16[48,10,384]{2,1,0:T(8,128)(2,1)S(1)}, u32[]{:S(2)}, u32[]{:S(2)}) async-start(bf16[48,10,384]{2,1,0:T(8,128)(2,1)} %reshape.75), calls=%async_computation.2 | async-start | bytes 1179648 | tf_op jit(solution)/shard_map/all_to_all | solution.py:82
Sparse Core Ops, SparseCore 0:
  60.7 45.1 all-gather.1
  166.9 82.9 reduce-scatter.1
where the time goes:
time: 303 us; the launch traced here: 298 us
  waiting for transfers between devices  123 us (41%)
  blocking collectives  73.7 us (24%)
  local copies, waits for them, and re-layouts  40.3 us (13%)
  matrix products  21.9 us (7%)
  starting transfers between devices  14.2 us (5%)
  between operations  13.5 us (4%)
  other arithmetic  11.5 us (4%)
    reduce_scatter x1, waiting for transfers between devices, one_scatter(): lax.psum_scatter(lines, axis, tiled=True).reshape(-1)  83.1 us
    all_to_all x1, blocking collectives, local(): lax.all_to_all(buckets, 'ep', split_axis=0, concat_axis=0, tiled=True)  48.1 us
    all_gather x1, blocking collectives, local(): lax.all_gather(tokens, 'tp', axis=1, tiled=True)  25.6 us
    all_to_all x1, waiting for transfers between devices, local(): lax.all_to_all(routed_sum.astype(jnp.bfloat16), 'ep', split_axis=0, conca...  23.6 us
    all_gather x1, waiting for transfers between devices, local(): lax.all_gather(received, 'tp', axis=2, tiled=True)  16.5 us
    all_to_all x1, starting transfers between devices, local(): lax.all_to_all(routed_sum.astype(jnp.bfloat16), 'ep', split_axis=0, conca...  14.2 us
    dot_general x2, matrix products, full_pass(): jnp.dot(hidden, w_down, preferred_element_type=jnp.float32)  14.1 us
    reshape x1, local copies, waits for them, and re-layouts, one_scatter(): lines = jnp.concatenate([b.reshape(length, -1) for b in tiles], axis=1)  11.4 us
  transfers between devices with their start and end apart: 3, of which 3 were waited for; matrix products, arithmetic and copies ran while one was open for 1% of the time, Pallas kernels for 0%

commit v1 on v0

v1 whole, which is shorter than its diff:
```python
import jax
import jax.numpy as jnp
from jax import lax
from jax.experimental import pallas as pl
from jax.experimental.pallas import tpu as pltpu
from jax.sharding import Mesh
from jax.sharding import PartitionSpec as P

LANES = 128


def slot_table(expert_ids, gate_scores, experts, copies):
    rows = expert_ids.shape[0]
    hit = expert_ids.T[None, :, :] == jnp.arange(experts, dtype=jnp.int32)[:, None, None]
    named = jnp.sum(hit.astype(jnp.float32), axis=1)
    score = jnp.sum(jnp.where(hit, gate_scores.T[None, :, :], 0.0), axis=1)
    earlier = jnp.arange(rows)[:, None] < jnp.arange(rows)[None, :]
    same = jnp.arange(rows)[:, None] == jnp.arange(rows)[None, :]
    weight = jnp.tile(earlier.astype(jnp.bfloat16) + 128 * same.astype(jnp.bfloat16), (1, copies))
    slot = jnp.dot(named.astype(jnp.bfloat16), weight, preferred_element_type=jnp.float32) - 128
    return slot.astype(jnp.int32), jnp.tile(score, (1, copies))


def ffn_kernel(steps, routed_rows, x, wg, wgp, wu, wup, sg, su, wd, wdp, sd, out, acc, sacc, hid, shid):
    i = pl.program_id(0)

    def wide(ref):
        parts = [
            jnp.concatenate([ref[p, j] for j in range(ref.shape[1])], axis=1) for p in range(ref.shape[0])
        ]
        return jnp.concatenate(parts, axis=1)

    @pl.when(i == 0)
    def _():
        acc[...] = jnp.zeros_like(acc)
        sacc[...] = jnp.zeros_like(sacc)

    @pl.when(i < steps)
    def _():
        rows = wide(x)
        w = jnp.concatenate([wg[...], wgp[...], wu[...], wup[...]], axis=1)
        acc[...] += jnp.dot(rows[:routed_rows], w, preferred_element_type=jnp.float32)
        ws = jnp.concatenate([sg[...], su[...]], axis=1)
        sacc[...] += jnp.dot(rows[routed_rows:], ws, preferred_element_type=jnp.float32)

    @pl.when(i == steps)
    def _():
        half = acc.shape[1] // 2
        hid[...] = (jax.nn.silu(acc[:, :half]) * acc[:, half:]).astype(jnp.bfloat16)
        shalf = sacc.shape[1] // 2
        shid[...] = (jax.nn.silu(sacc[:, :shalf]) * sacc[:, shalf:]).astype(jnp.bfloat16)

    @pl.when(i >= steps)
    def _():
        w = jnp.concatenate([wd[...], wdp[...]], axis=0)
        y = jnp.dot(hid[...], w, preferred_element_type=jnp.float32).astype(jnp.bfloat16)
        ys = jnp.dot(shid[...], sd[...], preferred_element_type=jnp.float32).astype(jnp.bfloat16)
        chunks = out.shape[1]
        for p in range(out.shape[0]):
            for j in range(chunks):
                at = (p * chunks + j) * LANES
                out[p, j, :routed_rows] = y[:, at : at + LANES]
                out[p, j, routed_rows:] = ys[:, at : at + LANES]


def ffn(x, own, partner, shared, routed_rows):
    chips, chunks, rows, _ = x.shape
    hidden = own[0].shape[1]
    per = 2
    steps = chips // per
    wide = per * chunks * LANES
    first = lambda i: jnp.minimum(i, steps - 1)
    second = lambda i: jnp.maximum(i - steps, 0)
    w_in = pl.BlockSpec((wide, hidden), lambda i: (first(i), 0))
    w_out = pl.BlockSpec((hidden, wide), lambda i: (0, second(i)))
    x_in = pl.BlockSpec((per, chunks, rows, LANES), lambda i: (first(i), 0, 0, 0))
    x_out = pl.BlockSpec((per, chunks, rows, LANES), lambda i: (second(i), 0, 0, 0))
    shared_rows = rows - routed_rows

    def body(*refs):
        ffn_kernel(steps, routed_rows, *refs)

    return pl.pallas_call(
        body,
        grid=(2 * steps,),
        in_specs=[x_in, w_in, w_in, w_in, w_in, w_in, w_in, w_out, w_out, w_out],
        out_specs=x_out,
        out_shape=jax.ShapeDtypeStruct(x.shape, jnp.bfloat16),
        scratch_shapes=[
            pltpu.VMEM((routed_rows, 4 * hidden), jnp.float32),
            pltpu.VMEM((shared_rows, 2 * hidden), jnp.float32),
            pltpu.VMEM((routed_rows, 2 * hidden), jnp.bfloat16),
            pltpu.VMEM((shared_rows, hidden), jnp.bfloat16),
        ],
        compiler_params=pltpu.CompilerParams(
            dimension_semantics=("arbitrary",), vmem_limit_bytes=48 * 1024 * 1024
        ),
        name="ffn",
    )(x, own[0], partner[0], own[1], partner[1], shared[0], shared[1], own[2], partner[2], shared[2])


def local(
    tokens,
    expert_ids,
    gate_scores,
    routed_gate,
    routed_up,
    routed_down,
    shared_gate,
    shared_up,
    shared_down,
):
    experts = routed_gate.shape[0] * lax.axis_size("ep")
    chips = lax.axis_size("t")
    core = lax.axis_index("c")
    row_count, top_count = expert_ids.shape
    capacity = min(row_count, row_count * top_count * 15 // (8 * experts))
    slots = capacity // 2
    swap = [(0, 1), (1, 0)]
    own = (routed_gate[0], routed_up[0], routed_down[0])
    partner = tuple(lax.ppermute(w, "c", swap) for w in own)

    width = 2 * tokens.shape[1]
    chunks = width // LANES
    message = -(-chunks * slots // 8) * 8
    pair = lax.all_gather(tokens, "c", axis=1, tiled=True)
    stacked = jnp.moveaxis(pair.reshape(row_count, chunks, LANES), 1, 0)
    slot, score = slot_table(expert_ids, gate_scores, experts, chunks)
    place = jnp.arange(message, dtype=jnp.int32)[:, None]
    column = jnp.arange(chunks * row_count, dtype=jnp.int32)[None, :]
    fits = (place // slots == column // row_count) & (place < chunks * slots)
    target = jnp.where(fits, place % slots + slots * core, -1024)
    match = slot[:, None, :] == target[None, :, :]
    select = match.astype(jnp.bfloat16).reshape(experts * message, chunks * row_count)
    buckets = jnp.dot(
        select, stacked.reshape(chunks * row_count, LANES), preferred_element_type=jnp.float32
    ).astype(jnp.bfloat16)
    received = lax.all_to_all(
        buckets.reshape(experts, message, LANES), "ep", split_axis=0, concat_axis=0, tiled=True
    )

    routed_rows = slots * experts
    rows = jnp.swapaxes(received, 0, 1)[: chunks * slots].reshape(chunks, routed_rows, LANES)
    block = jnp.concatenate([rows, stacked], axis=1)
    whole = lax.all_to_all(
        jnp.broadcast_to(block[None], (chips,) + block.shape), "t", split_axis=0, concat_axis=0, tiled=True
    )
    partial = ffn(whole, own, partner, (shared_gate, shared_up, shared_down), routed_rows)
    parts = lax.all_to_all(partial, "t", split_axis=0, concat_axis=0, tiled=True)
    total = jnp.sum(parts.astype(jnp.float32), axis=0)

    outcome = total[:, :routed_rows].astype(jnp.bfloat16).reshape(chunks * slots, experts, LANES)
    outcome = jnp.pad(outcome, ((0, message - chunks * slots), (0, 0), (0, 0)))
    returned = lax.all_to_all(
        jnp.swapaxes(outcome, 0, 1), "ep", split_axis=0, concat_axis=0, tiled=True
    ).reshape(experts * message, LANES)
    weights = jnp.where(match, score[:, None, :], 0.0).reshape(experts * message, chunks * row_count)
    routed = lax.dot_general(
        weights,
        returned.astype(jnp.float32),
        (((0,), (0,)), ((), ())),
        precision=lax.Precision.HIGHEST,
        preferred_element_type=jnp.float32,
    ).reshape(chunks, row_count, LANES)
    both = (routed + total[:, routed_rows:]).reshape(2, chunks // 2, row_count, LANES)
    mine = lax.dynamic_index_in_dim(both, core, 0, keepdims=False)
    other = lax.dynamic_index_in_dim(both, 1 - core, 0, keepdims=False)
    result = mine + lax.ppermute(other, "c", swap)
    return jnp.moveaxis(result, 0, 1).reshape(row_count, tokens.shape[1]).astype(jnp.bfloat16)


def solution(mesh):
    ep, tp = mesh.shape["ep"], mesh.shape["tp"]
    fine = Mesh(mesh.devices.reshape(ep, tp // 2, 2), ("ep", "t", "c"))
    tp_axes = ("t", "c")
    placed = (
        P("ep", tp_axes),
        P("ep", None),
        P("ep", None),
        P("ep", None, tp_axes),
        P("ep", None, tp_axes),
        P("ep", tp_axes, None),
        P(None, tp_axes),
        P(None, tp_axes),
        P(tp_axes, None),
    )
    return jax.shard_map(
        local, mesh=fine, in_specs=placed, out_specs=P("ep", tp_axes), check_vma=False
    )
```

time: 303 us -> 188 us (0.62); the launches traced: 298 us -> 187 us
  waiting for transfers between devices: 123 us -> 43.5 us
  local copies, waits for them, and re-layouts: 40.3 us -> 8.7 us
  matrix products: 21.9 us -> 2.11 us
  starting transfers between devices: 14.2 us -> 30.4 us
  blocking collectives: 73.7 us -> 89.8 us
  between operations: 13.5 us -> 0.24 us
  Pallas kernels: 0 us -> 10.2 us
  other arithmetic: 11.5 us -> 2.45 us
    reduce_scatter x1 -> x0, waiting for transfers between devices: 83.1 us -> none  [one_scatter(): lax.psum_scatter(lines, axis, tiled=True).reshape(-1)]
    all_to_all x1 -> x2, blocking collectives: 48.1 us -> 77.6 us  [the longest x1 44.9 us: local(): lax.all_to_all(partial, 't', split_axis=0, concat_axis=0, tiled=True)]
    reshape x7 -> x2, local copies, waits for them, and re-layouts: 29.5 us -> 0.18 us  [the longest x1 0.1 us: local(): total[:, :routed_rows].astype(jnp.bfloat16)]
    dot_general x6 -> x3, matrix products: 21.9 us -> 2.11 us  [the longest x1 1.56 us: local(): lax.dot_general(weights, returned.astype(jnp.float32), (((0,), (0,)), (()...]
    all_to_all x1 -> x2, waiting for transfers between devices: 23.6 us -> 41.7 us  [the longest x1 23.8 us: local(): lax.all_to_all(jnp.broadcast_to(block[None], (chips,) + block.shape), 't'...]
    ppermute x0 -> x4, starting transfers between devices: none -> 17.6 us  [the longest x3 9.72 us: local(): partner = tuple((lax.ppermute(w, 'c', swap) for w in own))]
    all_gather x1 -> x0, waiting for transfers between devices: 16.5 us -> none  [local(): lax.all_gather(received, 'tp', axis=2, tiled=True)]
    all_gather x1, blocking collectives: 25.6 us -> 12.2 us  [local(): pair = lax.all_gather(tokens, 'c', axis=1, tiled=True)]
  transfers between devices with their start and end apart: 3 -> 6, of which waited for: 3 -> 4; matrix products, arithmetic and copies ran while one was open for 1% -> 0% of each run, Pallas kernels for 0% -> 0%
where the time goes in v1:
time: 188 us; the launch traced here: 187 us
  blocking collectives  89.8 us (48%)
  waiting for transfers between devices  43.5 us (23%)
  starting transfers between devices  30.4 us (16%)
  Pallas kernels  10.2 us (5%)
  local copies, waits for them, and re-layouts  8.7 us (5%)
  other arithmetic  2.45 us (1%)
  matrix products  2.11 us (1%)
    all_to_all x1, blocking collectives, local(): lax.all_to_all(partial, 't', split_axis=0, concat_axis=0, tiled=True)  44.9 us
    all_to_all x1, blocking collectives, local(): lax.all_to_all(buckets.reshape(experts, message, LANES), 'ep', split_axis...  32.7 us
    all_to_all x1, waiting for transfers between devices, local(): lax.all_to_all(jnp.broadcast_to(block[None], (chips,) + block.shape), 't'...  23.8 us
    all_to_all x1, waiting for transfers between devices, local(): lax.all_to_all(jnp.swapaxes(outcome, 0, 1), 'ep', split_axis=0, concat_ax...  17.9 us
    all_gather x1, blocking collectives, local(): pair = lax.all_gather(tokens, 'c', axis=1, tiled=True)  12.2 us
    pallas_call x1, Pallas kernels, ffn(): pl.pallas_call(body, grid=(2 * steps,), in_specs=[x_in, w_in, w_in, w_in,...  10.2 us
    ppermute x3, starting transfers between devices, local(): partner = tuple((lax.ppermute(w, 'c', swap) for w in own))  9.72 us
    all_to_all x1, starting transfers between devices, local(): lax.all_to_all(jnp.swapaxes(outcome, 0, 1), 'ep', split_axis=0, concat_ax...  8.05 us
  transfers between devices with their start and end apart: 6, of which 4 were waited for; matrix products, arithmetic and copies ran while one was open for 0% of the time, Pallas kernels for 0%

profile of v1, /device:TPU:1, one launch (start us, length us, event | category | flops | bytes accessed | tf_op | source)
XLA Modules:
  0.0 187.4 jit_solution(6549078238897563343)
XLA Ops:
  0.1 0.1 tile.18
  0.2 12.2 %all_gather.3 = bf16[32,768]{1,0:T(8,128)(2,1)S(1)} all-gather(bf16[32,384]{1,0:T(8,128)(2,1)} %param.9), channel_id=1, replica_groups=mesh['ep'=48,'t'=8,'c'=2] {'c'}, dimensions={1}, use_global_device_ids=true | all-gather | bytes 73728 | tf_op jit(solution)/shard_map/all_gather | solution.py:126
  12.3 0.1 reshape.217
  12.4 0.8 convert_reduce_fusion.1
  13.3 0.2 fusion
  13.5 0.1 and_select_fusion
  13.6 0.2 broadcast_compare_fusion
  13.8 0.4 convolution_convert_fusion
  14.1 32.7 %all_to_all.20 = bf16[48,32,128]{2,1,0:T(8,128)(2,1)S(1)} all-to-all(bf16[48,32,128]{2,1,0:T(8,128)(2,1)S(1)} %bitcast.54), channel_id=1, replica_groups=mesh['ep'=48,'t'=8,'c'=2] {'ep'}, dimensions={0} | all-to-all | bytes 786432 | tf_op jit(solution)/shard_map/all_to_all | solution.py:138
  46.8 0.1 copy.29
  47.0 2.2 %broadcast_in_dim.59 = bf16[8,6,272,128]{3,2,1,0:T(8,128)(2,1)} broadcast(bf16[6,272,128]{2,1,0:T(8,128)(2,1)S(1)} %pad_maximum_fusion), dimensions={1,2,3} | broadcast | bytes 3760128 | tf_op jit(solution)/shard_map/broadcast_in_dim | solution.py:146
  49.2 0.0 copy-start
  49.2 0.0 copy-start.1
  49.2 4.7 %all-to-all-start.1 = ((bf16[8,6,272,128]{3,2,1,0:T(8,128)(2,1)}), bf16[8,6,272,128]{3,2,1,0:T(8,128)(2,1)}, u32[]{:S(2)}, u32[]{:S(2)}) async-start(bf16[8,6,272,128]{3,2,1,0:T(8,128)(2,1)} %broadcast_in_dim.59), calls=%async_computation.1 | async-start | bytes 6684672 | tf_op jit(solution)/shard_map/all_to_all | solution.py:145
  53.9 0.0 copy-done
  53.9 5.4 %collective-permute-start = (bf16[6144,128]{1,0:T(8,128)(2,1)S(1)}, bf16[6144,128]{1,0:T(8,128)(2,1)S(1)}, u32[]{:S(2)}, u32[]{:S(2)}) collective-permute-start(bf16[6144,128]{1,0:T(8,128)(2,1)S(1)} %bitcast.45), channel_id=1, source_target_pairs={{0,1},{1,0},{2,3},{3,2},{4,5},{5,4},{6,7},{7,6},{8,9},{9,8},{10,11... | collective-permute-start | bytes 4718600 | tf_op jit(solution)/shard_map/ppermute | solution.py:121
  59.3 0.0 copy-done.1
  59.3 1.9 %collective-permute-start.1 = (bf16[6144,128]{1,0:T(8,128)(2,1)S(1)}, bf16[6144,128]{1,0:T(8,128)(2,1)S(1)}, u32[]{:S(2)}, u32[]{:S(2)}) collective-permute-start(bf16[6144,128]{1,0:T(8,128)(2,1)S(1)} %bitcast.47), channel_id=1, source_target_pairs={{0,1},{1,0},{2,3},{3,2},{4,5},{5,4},{6,7},{7,6},{8,9},{9,8},{10,11... | collective-permute-start | bytes 4718600 | tf_op jit(solution)/shard_map/ppermute | solution.py:121
  61.3 2.4 %collective-permute-start.2 = (bf16[128,6144]{1,0:T(8,128)(2,1)}, bf16[128,6144]{1,0:T(8,128)(2,1)}, u32[]{:S(2)}, u32[]{:S(2)}) collective-permute-start(bf16[128,6144]{1,0:T(8,128)(2,1)} %bitcast.51), channel_id=1, source_target_pairs={{0,1},{1,0},{2,3},{3,2},{4,5},{5,4},{6,7},{7,6},{8,9},{9,8},{10,11... | collective-permute-start | bytes 4718600 | tf_op jit(solution)/shard_map/ppermute | solution.py:121
  63.7 0.0 collective-permute-done.refs_2_
  63.7 0.0 copy-start.2
  63.7 1.1 copy-done.2
  64.8 0.0 collective-permute-done.1.refs_4_
  64.8 0.0 copy-start.5
  64.8 1.2 copy-done.5
  66.1 1.0 collective-permute-done.2.refs_8_
  67.0 23.8 %all-to-all-done.1.refs_0_ = bf16[8,6,272,128]{3,2,1,0:T(8,128)(2,1)} async-done(((bf16[8,6,272,128]{3,2,1,0:T(8,128)(2,1)}), bf16[8,6,272,128]{3,2,1,0:T(8,128)(2,1)}, u32[]{:S(2)}, u32[]{:S(2)}) %all-to-all-start.1) | async-done | bytes 3342368 | tf_op jit(solution)/shard_map/all_to_all | solution.py:145
  90.9 0.0 copy-start.3
  90.9 1.4 copy-done.3
  92.3 10.2 %ffn.1 = bf16[8,6,272,128]{3,2,1,0:T(8,128)(2,1)} custom-call(bf16[8,6,272,128]{3,2,1,0:T(8,128)(2,1)} %all-to-all-done.1.refs_0_, bf16[6144,128]{1,0:T(8,128)(2,1)S(1)} %bitcast.46, bf16[6144,128]{1,0:T(8,128)(2,1)S(1)} %copy-done.3, bf16[6144,128]{1,0:T(8,128)(2,1)S(1)} %bitcast.48, bf16[6144,128]{1,0:T(8,128)(2,1)} %copy-done.5, ...), custom_call_target="tpu_custom_call" | custom-call | tf_op jit(solution)/shard_map/ffn/pallas_call | solution.py:83
  102.5 44.9 %all_to_all.21 = bf16[8,6,272,128]{3,2,1,0:T(8,128)(2,1)S(1)} all-to-all(bf16[8,6,272,128]{3,2,1,0:T(8,128)(2,1)} %ffn.1), channel_id=1, replica_groups=mesh['ep'=48,'t'=8,'c'=2] {'t'}, dimensions={0} | all-to-all | bytes 6684672 | tf_op jit(solution)/shard_map/all_to_all | solution.py:149
  147.4 0.5 convert_reduce_fusion
  147.8 0.0 copy-start.4
  147.9 0.9 copy-done.4
  148.7 0.1 slice.18
  148.8 0.1 copy.31
  148.9 0.8 pad_bitcast_fusion
  149.7 8.0 %all-to-all-start.3 = ((bf16[48,32,128]{2,1,0:T(8,128)(2,1)}), bf16[48,32,128]{2,1,0:T(8,128)(2,1)S(1)}, u32[]{:S(2)}, u32[]{:S(2)}) async-start(bf16[48,32,128]{2,1,0:T(8,128)(2,1)} %pad_bitcast_fusion), calls=%async_computation.3 | async-start | bytes 786432 | tf_op jit(solution)/shard_map/all_to_all | solution.py:154
  157.8 0.1 copy.26
  157.9 0.2 broadcast_select_fusion
  158.1 0.5 copy.27
  158.5 17.9 %all-to-all-done.3 = bf16[48,32,128]{2,1,0:T(8,128)(2,1)S(1)} async-done(((bf16[48,32,128]{2,1,0:T(8,128)(2,1)}), bf16[48,32,128]{2,1,0:T(8,128)(2,1)S(1)}, u32[]{:S(2)}, u32[]{:S(2)}) %all-to-all-start.3) | async-done | bytes 393248 | tf_op jit(solution)/shard_map/all_to_all | solution.py:154
  176.4 1.6 slice_add_fusion
  178.0 7.9 %collective-permute-start.3 = (f32[3,32,128]{2,1,0:T(8,128)S(1)}, f32[3,32,128]{2,1,0:T(8,128)S(1)}, u32[]{:S(2)}, u32[]{:S(2)}) collective-permute-start(f32[3,32,128]{2,1,0:T(8,128)S(1)} %dynamic-slice_bitcast_fusion), channel_id=1, source_target_pairs={{0,1},{1,0},{2,3},{3,2},{4,5},{5,4},{6,7},{7,6},{8,9},{9,8},{10,11... | collective-permute-start | bytes 147464 | tf_op jit(solution)/shard_map/ppermute | solution.py:168
  185.9 0.9 collective-permute-done.3
  186.8 0.6 copy_bitcast_fusion
  (9 shorter events, 0.1 us)
Async XLA Ops:
  49.2 4.7 %copy-start = (bf16[1,6144,128]{2,1,0:T(8,128)(2,1)S(1)}, bf16[1,6144,128]{2,1,0:T(8,128)(2,1)}, u32[]{:S(2)}) copy-start(bf16[1,6144,128]{2,1,0:T(8,128)(2,1)} %param.12) | copy-start | bytes 4718596
  49.2 10.1 %copy-start.1 = (bf16[1,6144,128]{2,1,0:T(8,128)(2,1)S(1)}, bf16[1,6144,128]{2,1,0:T(8,128)(2,1)}, u32[]{:S(2)}) copy-start(bf16[1,6144,128]{2,1,0:T(8,128)(2,1)} %param.13) | copy-start | bytes 4718596
  49.2 41.7 %all-to-all-start.1 = ((bf16[8,6,272,128]{3,2,1,0:T(8,128)(2,1)}), bf16[8,6,272,128]{3,2,1,0:T(8,128)(2,1)}, u32[]{:S(2)}, u32[]{:S(2)}) async-start(bf16[8,6,272,128]{3,2,1,0:T(8,128)(2,1)} %broadcast_in_dim.59), calls=%async_computation.1 | async-start | bytes 6684672 | tf_op jit(solution)/shard_map/all_to_all | solution.py:145
  53.9 9.8 %collective-permute-start = (bf16[6144,128]{1,0:T(8,128)(2,1)S(1)}, bf16[6144,128]{1,0:T(8,128)(2,1)S(1)}, u32[]{:S(2)}, u32[]{:S(2)}) collective-permute-start(bf16[6144,128]{1,0:T(8,128)(2,1)S(1)} %bitcast.45), channel_id=1, source_target_pairs={{0,1},{1,0},{2,3},{3,2},{4,5},{5,4},{6,7},{7,6},{8,9},{9,8},{10,11... | collective-permute-start | bytes 4718600 | tf_op jit(solution)/shard_map/ppermute | solution.py:121
  59.3 5.5 %collective-permute-start.1 = (bf16[6144,128]{1,0:T(8,128)(2,1)S(1)}, bf16[6144,128]{1,0:T(8,128)(2,1)S(1)}, u32[]{:S(2)}, u32[]{:S(2)}) collective-permute-start(bf16[6144,128]{1,0:T(8,128)(2,1)S(1)} %bitcast.47), channel_id=1, source_target_pairs={{0,1},{1,0},{2,3},{3,2},{4,5},{5,4},{6,7},{7,6},{8,9},{9,8},{10,11... | collective-permute-start | bytes 4718600 | tf_op jit(solution)/shard_map/ppermute | solution.py:121
  61.3 5.8 %collective-permute-start.2 = (bf16[128,6144]{1,0:T(8,128)(2,1)}, bf16[128,6144]{1,0:T(8,128)(2,1)}, u32[]{:S(2)}, u32[]{:S(2)}) collective-permute-start(bf16[128,6144]{1,0:T(8,128)(2,1)} %bitcast.51), channel_id=1, source_target_pairs={{0,1},{1,0},{2,3},{3,2},{4,5},{5,4},{6,7},{7,6},{8,9},{9,8},{10,11... | collective-permute-start | bytes 4718600 | tf_op jit(solution)/shard_map/ppermute | solution.py:121
  63.7 1.1 copy-start.2
  64.8 1.2 copy-start.5
  90.9 1.4 copy-start.3
  147.8 0.9 copy-start.4
  149.7 26.7 %all-to-all-start.3 = ((bf16[48,32,128]{2,1,0:T(8,128)(2,1)}), bf16[48,32,128]{2,1,0:T(8,128)(2,1)S(1)}, u32[]{:S(2)}, u32[]{:S(2)}) async-start(bf16[48,32,128]{2,1,0:T(8,128)(2,1)} %pad_bitcast_fusion), calls=%async_computation.3 | async-start | bytes 786432 | tf_op jit(solution)/shard_map/all_to_all | solution.py:154
  178.0 8.8 %collective-permute-start.3 = (f32[3,32,128]{2,1,0:T(8,128)S(1)}, f32[3,32,128]{2,1,0:T(8,128)S(1)}, u32[]{:S(2)}, u32[]{:S(2)}) collective-permute-start(f32[3,32,128]{2,1,0:T(8,128)S(1)} %dynamic-slice_bitcast_fusion), channel_id=1, source_target_pairs={{0,1},{1,0},{2,3},{3,2},{4,5},{5,4},{6,7},{7,6},{8,9},{9,8},{10,11... | collective-permute-start | bytes 147464 | tf_op jit(solution)/shard_map/ppermute | solution.py:168

commit v2 on v1

v2 whole, which is shorter than its diff:
```python
import jax
import jax.numpy as jnp
from jax import lax
from jax.experimental import pallas as pl
from jax.experimental.pallas import tpu as pltpu
from jax.sharding import Mesh
from jax.sharding import PartitionSpec as P


LANES = 128
PARAMS = pltpu.CompilerParams(dimension_semantics=("arbitrary",), vmem_limit_bytes=60 * 1024 * 1024)


def slot_table(expert_ids, gate_scores, experts, copies):
    rows = expert_ids.shape[0]
    hit = expert_ids.T[None, :, :] == jnp.arange(experts, dtype=jnp.int32)[:, None, None]
    named = jnp.sum(hit.astype(jnp.float32), axis=1)
    score = jnp.sum(jnp.where(hit, gate_scores.T[None, :, :], 0.0), axis=1)
    earlier = jnp.arange(rows)[:, None] < jnp.arange(rows)[None, :]
    same = jnp.arange(rows)[:, None] == jnp.arange(rows)[None, :]
    weight = jnp.tile(earlier.astype(jnp.bfloat16) + 128 * same.astype(jnp.bfloat16), (1, copies))
    slot = jnp.dot(named.astype(jnp.bfloat16), weight, preferred_element_type=jnp.float32) - 128
    return slot.astype(jnp.int32), jnp.tile(score, (1, copies))


def activate(total):
    half = total.shape[1] // 2
    return (jax.nn.silu(total[:, :half]) * total[:, half:]).astype(jnp.bfloat16)


def estimate(flops):
    return pl.CostEstimate(flops=flops, bytes_accessed=flops // 400, transcendentals=0)


def split_weights(y, w_gate, w_up, w_down, count, width):
    hidden = w_gate.shape[1]

    def body(_, gm, go, um, uo, dm, do, mine, other, mine_down, other_down):
        mine[0] = gm[...]
        mine[1] = um[...]
        other[0] = go[...]
        other[1] = uo[...]
        mine_down[...] = dm[...]
        other_down[...] = do[...]

    near = pl.BlockSpec((width, hidden), lambda i, y: (2 * i + y[0], 0))
    far = pl.BlockSpec((width, hidden), lambda i, y: (2 * i + 1 - y[0], 0))
    near_down = pl.BlockSpec((hidden, width), lambda i, y: (0, 2 * i + y[0]))
    far_down = pl.BlockSpec((hidden, width), lambda i, y: (0, 2 * i + 1 - y[0]))
    pair = pl.BlockSpec((2, width, hidden), lambda i, y: (0, i, 0))
    column = pl.BlockSpec((hidden, width), lambda i, y: (0, i))
    pair_shape = jax.ShapeDtypeStruct((2, count * width, hidden), w_gate.dtype)
    column_shape = jax.ShapeDtypeStruct((hidden, count * width), w_gate.dtype)
    return pl.pallas_call(
        body,
        grid_spec=pltpu.PrefetchScalarGridSpec(
            num_scalar_prefetch=1,
            grid=(count,),
            in_specs=[near, far, near, far, near_down, far_down],
            out_specs=[pair, pair, column, column],
        ),
        out_shape=[pair_shape, pair_shape, column_shape, column_shape],
        cost_estimate=estimate(10**9),
        compiler_params=PARAMS,
        name="split",
    )(y[None], w_gate, w_gate, w_up, w_up, w_down, w_down)


def partial_sums(x, ins):
    chips, chunks, rows, _ = x.shape
    hidden = ins[0].shape[2]
    width = chunks * LANES
    wide = 2 * len(ins) * hidden

    def body(x_ref, *refs):
        w, acc, sent = refs[: len(ins)], refs[-2], refs[-1]
        i = pl.program_id(0)

        @pl.when(i == 0)
        def _():
            acc[...] = jnp.zeros_like(acc)

        lines = jnp.concatenate([x_ref[0, j] for j in range(chunks)], axis=1)
        weights = jnp.concatenate([r[k] for k in range(2) for r in w], axis=1)
        acc[...] += jnp.dot(lines, weights, preferred_element_type=jnp.float32)

        @pl.when(i == chips - 1)
        def _():
            sent[...] = acc[...].astype(sent.dtype)

    whole = pl.BlockSpec((rows, wide), lambda i: (0, 0))
    return pl.pallas_call(
        body,
        grid=(chips,),
        in_specs=[pl.BlockSpec((1, chunks, rows, LANES), lambda i: (i, 0, 0, 0))]
        + [pl.BlockSpec((2, width, hidden), lambda i: (0, i, 0))] * len(ins),
        out_specs=[whole, whole],
        out_shape=[
            jax.ShapeDtypeStruct((rows, wide), jnp.float32),
            jax.ShapeDtypeStruct((rows, wide), jnp.bfloat16),
        ],
        cost_estimate=estimate(2 * rows * chips * width * wide),
        compiler_params=PARAMS,
        name="partial",
    )(x, *ins)


def down(sums, other, outs, count, chunks):
    rows, wide = sums.shape
    part = outs[0].shape[0]
    width = chunks * LANES

    def body(s_ref, o_ref, *refs):
        w, out, h = refs[: len(outs)], refs[-2], refs[-1]

        @pl.when(pl.program_id(0) == 0)
        def _():
            theirs = o_ref[...].astype(jnp.float32)
            quarter = wide // 4
            order = [1, 0, 3, 2]
            theirs = jnp.concatenate([theirs[:, q * quarter : (q + 1) * quarter] for q in order], axis=1)
            h[...] = activate(s_ref[...] + theirs)

        weights = jnp.concatenate([r[...] for r in w], axis=0)
        result = jnp.dot(h[...], weights, preferred_element_type=jnp.float32)
        for j in range(chunks):
            out[0, j] = result[:, j * LANES : (j + 1) * LANES].astype(out.dtype)

    whole = pl.BlockSpec((rows, wide), lambda i: (0, 0))
    return pl.pallas_call(
        body,
        grid=(count,),
        in_specs=[whole, whole] + [pl.BlockSpec((part, width), lambda i: (0, i))] * len(outs),
        out_specs=pl.BlockSpec((1, chunks, rows, LANES), lambda i: (i, 0, 0, 0)),
        out_shape=jax.ShapeDtypeStruct((count, chunks, rows, LANES), jnp.bfloat16),
        scratch_shapes=[pltpu.VMEM((rows, wide // 2), jnp.bfloat16)],
        cost_estimate=estimate(2 * rows * count * width * 4 * part),
        compiler_params=PARAMS,
        name="down",
    )(sums, other, *outs)


def shared_expert(x, at, w_gate, w_up, w_down):
    pairs, ys, chunks, rows, _ = x.shape
    hidden = w_gate.shape[1]
    width = ys * chunks * LANES

    def body(_, x_ref, g_ref, u_ref, d_ref, out, acc, h):
        i = pl.program_id(0)

        @pl.when(i == 0)
        def _():
            acc[...] = jnp.zeros_like(acc)

        @pl.when(i < pairs)
        def _():
            lines = jnp.concatenate([x_ref[0, y, j] for y in range(ys) for j in range(chunks)], axis=1)
            weights = jnp.concatenate([g_ref[...], u_ref[...]], axis=1)
            acc[...] += jnp.dot(lines, weights, preferred_element_type=jnp.float32)

        @pl.when(i == pairs)
        def _():
            h[...] = activate(acc[...])

        @pl.when(i >= pairs)
        def _():
            result = jnp.dot(h[...], d_ref[...], preferred_element_type=jnp.float32)
            for y in range(ys):
                for j in range(chunks):
                    lane = (y * chunks + j) * LANES
                    out[0, y, j] = result[:, lane : lane + LANES].astype(out.dtype)

    first = lambda i: jnp.minimum(i, pairs - 1)
    second = lambda i: jnp.maximum(i - pairs, 0)
    w_in = pl.BlockSpec((width, hidden), lambda i, at: (at[first(i)], 0))
    block = (1, ys, chunks, rows, LANES)
    return pl.pallas_call(
        body,
        grid_spec=pltpu.PrefetchScalarGridSpec(
            num_scalar_prefetch=1,
            grid=(2 * pairs,),
            in_specs=[
                pl.BlockSpec(block, lambda i, at: (first(i), 0, 0, 0, 0)),
                w_in,
                w_in,
                pl.BlockSpec((hidden, width), lambda i, at: (0, at[second(i)])),
            ],
            out_specs=pl.BlockSpec(block, lambda i, at: (second(i), 0, 0, 0, 0)),
            scratch_shapes=[pltpu.VMEM((rows, 2 * hidden), jnp.float32), pltpu.VMEM((rows, hidden), jnp.bfloat16)],
        ),
        out_shape=jax.ShapeDtypeStruct(x.shape, jnp.bfloat16),
        cost_estimate=estimate(6 * rows * pairs * width * hidden),
        compiler_params=PARAMS,
        name="shared",
    )(at, x, w_gate, w_up, w_down)


def local(
    tokens,
    expert_ids,
    gate_scores,
    routed_gate,
    routed_up,
    routed_down,
    shared_gate,
    shared_up,
    shared_down,
):
    experts = routed_gate.shape[0] * lax.axis_size("ep")
    xs = lax.axis_size("x")
    core, xi, yi = lax.axis_index("c"), lax.axis_index("x"), lax.axis_index("y")
    row_count, top_count = expert_ids.shape
    capacity = min(row_count, row_count * top_count * 15 // (8 * experts))
    slots = capacity // 2
    swap = [(0, 1), (1, 0)]

    def to_y(v):
        return lax.ppermute(v, "y", swap)

    def to_x(v, bit):
        return lax.ppermute(v, "x", [(i, i ^ bit) for i in range(xs)])

    def to_c(v):
        return lax.ppermute(v, "c", swap)

    def halve(v, bit):
        half = v.shape[0] // 2
        return (v[:half].astype(jnp.float32) + to_x(v[half:], bit).astype(jnp.float32)).astype(v.dtype)

    def exchange(v, axes):
        return lax.all_to_all(v, axes, split_axis=0, concat_axis=0, tiled=True)

    chunks = 2 * tokens.shape[1] // LANES
    used = chunks * slots
    message = -(-used // 8) * 8
    columns = chunks * row_count
    routed_rows = slots * experts
    width = chunks * LANES

    pair = lax.all_gather(tokens, "c", axis=1, tiled=True)
    stacked = jnp.moveaxis(pair.reshape(row_count, chunks, LANES), 1, 0)
    slot, score = slot_table(expert_ids, gate_scores, experts, chunks)
    place = jnp.arange(message, dtype=jnp.int32)[:, None]
    column = jnp.arange(columns, dtype=jnp.int32)[None, :]
    fits = (place // slots == column // row_count) & (place < used)
    target = jnp.where(fits, place % slots + slots * core, -1024)
    match = slot[:, None, :] == target[None, :, :]
    select = match.astype(jnp.bfloat16).reshape(experts * message, columns)
    buckets = jnp.dot(select, stacked.reshape(columns, LANES), preferred_element_type=jnp.float32)
    buckets = buckets.astype(jnp.bfloat16).reshape(experts, message, LANES)
    received = exchange(buckets, "ep")

    _, w_gate, w_up, w_down, ours = lax.optimization_barrier(
        (buckets, routed_gate[0], routed_up[0], routed_down[0], stacked)
    )
    theirs = to_y(ours)
    mine, other, mine_down, other_down = split_weights(yi, w_gate, w_up, w_down, xs, width)
    got = to_y(other)
    partner = to_c(mine)
    partner_down = to_c(mine_down)
    whole = jnp.where(yi == 0, jnp.stack([ours, theirs]), jnp.stack([theirs, ours]))[None]
    whole = jnp.concatenate([whole, to_x(whole, 2)], axis=0)
    received, partner, partner_down, whole = lax.optimization_barrier(
        (received, partner, partner_down, whole)
    )
    rows = jnp.swapaxes(received, 0, 1)[:used].reshape(chunks, routed_rows, LANES)
    gathered = exchange(jnp.broadcast_to(rows[None], (xs,) + rows.shape), "x")
    got_down = to_y(other_down)
    partner_got = to_c(got)
    gathered, partner_got = lax.optimization_barrier((gathered, partner_got))
    sums, sent = partial_sums(gathered, (mine, partner, got, partner_got))
    other_sums = to_y(sent)
    whole = jnp.concatenate([whole, to_x(whole, 1)], axis=0)
    partner_got_down = to_c(got_down)
    other_sums, partner_got_down, whole = lax.optimization_barrier((other_sums, partner_got_down, whole))
    products = down(sums, other_sums, (mine_down, partner_down, got_down, partner_got_down), xs, chunks)
    reduced = exchange(products, "x")
    at = jnp.bitwise_xor(jnp.array([0, 2, 1, 3], jnp.int32), xi)
    part = shared_expert(whole, at, shared_gate, shared_up, shared_down)
    reduced, part = lax.optimization_barrier((reduced, part))
    total = jnp.sum(reduced.astype(jnp.float32), axis=0).astype(jnp.bfloat16)
    outcome = jnp.pad(total.reshape(used, experts, LANES), ((0, message - used), (0, 0), (0, 0)))
    returned = exchange(jnp.swapaxes(outcome, 0, 1), "ep")
    part = halve(part, 1)
    part = halve(part, 2)[0]
    kept = jnp.where(yi == 0, part[0], part[1])
    lost = jnp.where(yi == 0, part[1], part[0])
    shared = kept.astype(jnp.float32) + to_y(lost).astype(jnp.float32)
    returned, shared = lax.optimization_barrier((returned, shared))

    returned = returned.reshape(experts * message, LANES)
    weights = jnp.where(match, score[:, None, :], 0.0).reshape(experts * message, columns)
    routed = lax.dot_general(
        weights,
        returned.astype(jnp.float32),
        (((0,), (0,)), ((), ())),
        precision=lax.Precision.HIGHEST,
        preferred_element_type=jnp.float32,
    )
    both = (routed.reshape(shared.shape) + shared).reshape(2, chunks // 2, row_count, LANES)
    keep = jnp.where(core == 0, both[0], both[1])
    send = jnp.where(core == 0, both[1], both[0])
    result = keep + lax.ppermute(send, "c", swap)
    return jnp.moveaxis(result, 0, 1).reshape(row_count, tokens.shape[1]).astype(jnp.bfloat16)


def solution(mesh):
    ep, tp = mesh.shape["ep"], mesh.shape["tp"]
    fine = Mesh(mesh.devices.reshape(ep, tp // 4, 2, 2), ("ep", "x", "y", "c"))
    tp_axes = ("x", "y", "c")
    placed = (
        P("ep", tp_axes),
        P("ep", None),
        P("ep", None),
        P("ep", None, tp_axes),
        P("ep", None, tp_axes),
        P("ep", tp_axes, None),
        P(None, tp_axes),
        P(None, tp_axes),
        P(tp_axes, None),
    )
    return jax.shard_map(
        local, mesh=fine, in_specs=placed, out_specs=P("ep", tp_axes), check_vma=False
    )
```

time: 188 us -> 209 us (1.11)
  blocking collectives: 89.8 us -> 12.2 us
  starting transfers between devices: 30.4 us -> 74.4 us
  waiting for transfers between devices: 43.5 us -> 84.8 us
  Pallas kernels: 10.2 us -> 23.5 us
    all_to_all x2 -> x0, blocking collectives: 77.6 us -> none  [the longest x1 44.9 us: local(): lax.all_to_all(partial, 't', split_axis=0, concat_axis=0, tiled=True)]
    ppermute x4 -> x14, waiting for transfers between devices: 1.82 us -> 68.5 us  [the longest x5 54.9 us: to_y(): return lax.ppermute(v, 'y', swap)]
    all_to_all x2 -> x4, waiting for transfers between devices: 41.7 us -> 16.3 us  [exchange(): return lax.all_to_all(v, axes, split_axis=0, concat_axis=0, tiled=True)]
    ppermute x4 -> x14, starting transfers between devices: 17.6 us -> 41.7 us  [the longest x4 12.5 us: to_c(): return lax.ppermute(v, 'c', swap)]
    all_to_all x2 -> x4, starting transfers between devices: 12.8 us -> 32.6 us  [exchange(): return lax.all_to_all(v, axes, split_axis=0, concat_axis=0, tiled=True)]
    pallas_call x1 -> x4, Pallas kernels: 10.2 us -> 23.5 us  [the longest x1 7.03 us: shared_expert(): pl.pallas_call(body, grid_spec=pltpu.PrefetchScalarGridSpec(num_scalar_pr...]
  transfers between devices with their start and end apart: 6 -> 18, of which waited for: 4 -> 11; matrix products, arithmetic and copies ran while one was open for 0% -> 2% of each run, Pallas kernels for 0% -> 6%
where the time goes in v2:
time: 209 us; the launch traced here: 208 us
  waiting for transfers between devices  84.8 us (41%)
  starting transfers between devices  74.4 us (36%)
  Pallas kernels  23.5 us (11%)
  blocking collectives  12.2 us (6%)
  local copies, waits for them, and re-layouts  6.73 us (3%)
  other arithmetic  3.7 us (2%)
    ppermute x5, waiting for transfers between devices, to_y(): return lax.ppermute(v, 'y', swap)  54.9 us
    all_to_all x4, starting transfers between devices, exchange(): return lax.all_to_all(v, axes, split_axis=0, concat_axis=0, tiled=True)  32.6 us
    all_to_all x4, waiting for transfers between devices, exchange(): return lax.all_to_all(v, axes, split_axis=0, concat_axis=0, tiled=True)  16.3 us
    ppermute x4, waiting for transfers between devices, to_x(): return lax.ppermute(v, 'x', [(i, i ^ bit) for i in range(xs)])  12.7 us
    ppermute x4, starting transfers between devices, to_c(): return lax.ppermute(v, 'c', swap)  12.5 us
    all_gather x1, blocking collectives, local(): pair = lax.all_gather(tokens, 'c', axis=1, tiled=True)  12.2 us
    ppermute x4, starting transfers between devices, to_x(): return lax.ppermute(v, 'x', [(i, i ^ bit) for i in range(xs)])  11.1 us
    ppermute x5, starting transfers between devices, to_y(): return lax.ppermute(v, 'y', swap)  9.92 us
  transfers between devices with their start and end apart: 18, of which 11 were waited for; matrix products, arithmetic and copies ran while one was open for 2% of the time, Pallas kernels for 6%

profile of v2, /device:TPU:1, one launch (start us, length us, event | category | flops | bytes accessed | tf_op | source)
XLA Modules:
  0.0 207.7 jit_solution(6565739033986055312)
XLA Ops:
  0.2 12.2 %all_gather.3 = bf16[32,768]{1,0:T(8,128)(2,1)S(1)} all-gather(bf16[32,384]{1,0:T(8,128)(2,1)} %param.10), channel_id=1, replica_groups=mesh['ep'=48,'x'=4,'y'=2,'c'=2] {'c'}, dimensions={1}, use_global_device_ids=true | all-gather | bytes 73728 | tf_op jit(solution)/shard_map/all_gather | solution.py:240
  12.4 0.8 convert_reduce_fusion
  13.7 1.1 convolution_convert_fusion
  14.8 5.1 %split.1 = (bf16[2,3072,128]{2,1,0:T(8,128)(2,1)}, bf16[2,3072,128]{2,1,0:T(8,128)(2,1)}, bf16[128,3072]{1,0:T(8,128)(2,1)}, bf16[128,3072]{1,0:T(8,128)(2,1)}) custom-call(s32[1]{0:T(128)} %bitcast.10._, bf16[6144,128]{1,0:T(8,128)(2,1)} %bitcast.52, bf16[6144,128]{1,0:T(8,128)(2,1)} %bitcast.53, bf16[6144,128]{1,0:T(8,128)(2,1)} %bitcast.54, ...), custom_call_target="tpu_custom_call" | custom-call | flops 1000000000 | bytes 2500000 | tf_op jit(solution)/shard_map/split/pallas_call | solution.py:54
  20.0 1.9 collective-permute-start.4
  21.9 2.3 %collective-permute-start = (bf16[2,3072,128]{2,1,0:T(8,128)(2,1)}, bf16[2,3072,128]{2,1,0:T(8,128)(2,1)}, u32[]{:S(2)}, u32[]{:S(2)}) collective-permute-start(bf16[2,3072,128]{2,1,0:T(8,128)(2,1)} %get-tuple-element.31.refs_0_), channel_id=1, source_target_pairs={{0,1},{1,0},{2,3},{3,2},{4,5},{5,4},{6,7},{7,6},{8,9},{9,8},{10,11... | collective-permute-start | bytes 4718600 | tf_op jit(solution)/shard_map/ppermute | solution.py:224
  24.1 12.5 %all-to-all-start = ((bf16[48,32,128]{2,1,0:T(8,128)(2,1)}), bf16[48,32,128]{2,1,0:T(8,128)(2,1)S(1)}, u32[]{:S(2)}, u32[]{:S(2)}) async-start(bf16[48,32,128]{2,1,0:T(8,128)(2,1)} %bitcast.9), calls=%async_computation | async-start | bytes 786432 | tf_op jit(solution)/shard_map/all_to_all | solution.py:231
  36.7 2.2 %collective-permute-start.1 = (bf16[128,3072]{1,0:T(8,128)(2,1)}, bf16[128,3072]{1,0:T(8,128)(2,1)S(1)}, u32[]{:S(2)}, u32[]{:S(2)}) collective-permute-start(bf16[128,3072]{1,0:T(8,128)(2,1)} %get-tuple-element.32.refs_0_), channel_id=1, source_target_pairs={{0,1},{1,0},{2,3},{3,2},{4,5},{5,4},{6,7},{7,6},{8,9},{9,8},{10,11... | collective-permute-start | bytes 2359304 | tf_op jit(solution)/shard_map/ppermute | solution.py:224
  38.9 26.9 %collective-permute-done.4.refs_2_ = bf16[2,3072,128]{2,1,0:T(8,128)(2,1)S(1)} collective-permute-done((bf16[2,3072,128]{2,1,0:T(8,128)(2,1)}, bf16[2,3072,128]{2,1,0:T(8,128)(2,1)S(1)}, u32[]{:S(2)}, u32[]{:S(2)}) %collective-permute-start.4) | collective-permute-done | bytes 1572896 | tf_op jit(solution)/shard_map/ppermute | solution.py:218
  65.7 3.3 %collective-permute-start.5 = (bf16[2,3072,128]{2,1,0:T(8,128)(2,1)S(1)}, bf16[2,3072,128]{2,1,0:T(8,128)(2,1)}, u32[]{:S(2)}, u32[]{:S(2)}) collective-permute-start(bf16[2,3072,128]{2,1,0:T(8,128)(2,1)S(1)} %collective-permute-done.4.refs_2_), channel_id=1, source_target_pairs={{0,1},{1,0},{2,3},{3,2},{4,5},{5,4},{6,7},{7,6},{8,9},{9,8},{10,11... | collective-permute-start | bytes 4718600 | tf_op jit(solution)/shard_map/ppermute | solution.py:224
  69.0 1.9 collective-permute-start.2
  71.0 3.2 %collective-permute-done.2 = bf16[6,32,128]{2,1,0:T(8,128)(2,1)S(1)} collective-permute-done((bf16[6,32,128]{2,1,0:T(8,128)(2,1)S(1)}, bf16[6,32,128]{2,1,0:T(8,128)(2,1)S(1)}, u32[]{:S(2)}, u32[]{:S(2)}) %collective-permute-start.2) | collective-permute-done | bytes 49184 | tf_op jit(solution)/shard_map/ppermute | solution.py:218
  74.2 1.9 collective-permute-start.3
  76.1 4.9 %collective-permute-done.3 = bf16[1,2,6,32,128]{4,3,2,1,0:T(8,128)(2,1)S(1)} collective-permute-done((bf16[1,2,6,32,128]{4,3,2,1,0:T(8,128)(2,1)S(1)}, bf16[1,2,6,32,128]{4,3,2,1,0:T(8,128)(2,1)S(1)}, u32[]{:S(2)}, u32[]{:S(2)}) %collective-permute-start.3) | collective-permute-done | bytes 98336 | tf_op jit(solution)/shard_map/ppermute | solution.py:221
  81.1 0.8 copy-done.3
  82.1 1.3 broadcast_in_dim.66
  83.5 3.6 %all-to-all-start.1 = ((bf16[4,6,240,128]{3,2,1,0:T(8,128)(2,1)}), bf16[4,6,240,128]{3,2,1,0:T(8,128)(2,1)S(1)}, u32[]{:S(2)}, u32[]{:S(2)}) async-start(bf16[4,6,240,128]{3,2,1,0:T(8,128)(2,1)} %broadcast_in_dim.66), calls=%async_computation.1 | async-start | bytes 2949120 | tf_op jit(solution)/shard_map/all_to_all | solution.py:231
  87.0 1.9 collective-permute-start.7
  89.0 17.4 %collective-permute-done.7.refs_2_ = bf16[128,3072]{1,0:T(8,128)(2,1)} collective-permute-done((bf16[128,3072]{1,0:T(8,128)(2,1)}, bf16[128,3072]{1,0:T(8,128)(2,1)}, u32[]{:S(2)}, u32[]{:S(2)}) %collective-permute-start.7) | collective-permute-done | bytes 786464 | tf_op jit(solution)/shard_map/ppermute | solution.py:218
  106.3 4.8 %collective-permute-start.8 = (bf16[128,3072]{1,0:T(8,128)(2,1)}, bf16[128,3072]{1,0:T(8,128)(2,1)}, u32[]{:S(2)}, u32[]{:S(2)}) collective-permute-start(bf16[128,3072]{1,0:T(8,128)(2,1)} %collective-permute-done.7.refs_2_), channel_id=1, source_target_pairs={{0,1},{1,0},{2,3},{3,2},{4,5},{5,4},{6,7},{7,6},{8,9},{9,8},{10,11... | collective-permute-start | bytes 2359304 | tf_op jit(solution)/shard_map/ppermute | solution.py:224
  111.1 1.1 copy-done
  112.2 6.1 %partial.1 = (f32[240,1024]{1,0:T(8,128)}, bf16[240,1024]{1,0:T(8,128)(2,1)}) custom-call(bf16[4,6,240,128]{3,2,1,0:T(8,128)(2,1)} %copy-done, bf16[2,3072,128]{2,1,0:T(8,128)(2,1)} %get-tuple-element.31.refs_0_, bf16[2,3072,128]{2,1,0:T(8,128)(2,1)} %collective-permute-done.refs_1_, bf16[2,3072,128]{2,1,0:T(8,128)(2,1)} %copy-done.2, ...), custom_call_target="tpu_custom_call" | custom-call | flops 1509949440 | bytes 3774873 | tf_op jit(solution)/shard_map/partial/pallas_call | solution.py:92
  118.3 1.9 collective-permute-start.6
  120.2 3.3 %collective-permute-start.9 = (bf16[2,2,6,32,128]{4,3,2,1,0:T(8,128)(2,1)S(1)}, bf16[2,2,6,32,128]{4,3,2,1,0:T(8,128)(2,1)S(1)}, u32[]{:S(2)}, u32[]{:S(2)}) collective-permute-start(bf16[2,2,6,32,128]{4,3,2,1,0:T(8,128)(2,1)S(1)} %pad_maximum_fusion.1), channel_id=1, source_target_pairs={{0,4},{4,0},{8,12},{12,8},{1,5},{5,1},{9,13},{13,9},{2,6},{6,2},{1... | collective-permute-start | bytes 589832 | tf_op jit(solution)/shard_map/ppermute | solution.py:221
  123.5 4.7 %collective-permute-done.9 = bf16[2,2,6,32,128]{4,3,2,1,0:T(8,128)(2,1)S(1)} collective-permute-done((bf16[2,2,6,32,128]{4,3,2,1,0:T(8,128)(2,1)S(1)}, bf16[2,2,6,32,128]{4,3,2,1,0:T(8,128)(2,1)S(1)}, u32[]{:S(2)}, u32[]{:S(2)}) %collective-permute-start.9) | collective-permute-done | bytes 196640 | tf_op jit(solution)/shard_map/ppermute | solution.py:221
  128.3 0.8 pad_maximum_fusion.x_ref
  129.1 4.1 %collective-permute-done.6.o_ref = bf16[240,1024]{1,0:T(8,128)(2,1)S(1)} collective-permute-done((bf16[240,1024]{1,0:T(8,128)(2,1)}, bf16[240,1024]{1,0:T(8,128)(2,1)S(1)}, u32[]{:S(2)}, u32[]{:S(2)}) %collective-permute-start.6) | collective-permute-done | bytes 491552 | tf_op jit(solution)/shard_map/ppermute | solution.py:218
  133.2 0.8 copy-done.4
  134.0 5.3 %down.1 = bf16[4,6,240,128]{3,2,1,0:T(8,128)(2,1)} custom-call(f32[240,1024]{1,0:T(8,128)} %get-tuple-element.39.s_ref, bf16[240,1024]{1,0:T(8,128)(2,1)} %copy-done.4, bf16[128,3072]{1,0:T(8,128)(2,1)} %get-tuple-element.32.refs_0_, bf16[128,3072]{1,0:T(8,128)(2,1)} %copy-done.3, bf16[128,3072]{1,0:T(8,128)(2,1)} %collective-permute-done.7.refs_2_, ...), custom_call_target="tpu_custom_call" | custom-call | flops 754974720 | bytes 1887436 | tf_op jit(solution)/shard_map/down/pallas_call | solution.py:130
  139.3 4.3 %all-to-all-start.2 = ((bf16[4,6,240,128]{3,2,1,0:T(8,128)(2,1)}), bf16[4,6,240,128]{3,2,1,0:T(8,128)(2,1)S(1)}, u32[]{:S(2)}, u32[]{:S(2)}) async-start(bf16[4,6,240,128]{3,2,1,0:T(8,128)(2,1)} %down.1), calls=%async_computation.2 | async-start | bytes 2949120 | tf_op jit(solution)/shard_map/all_to_all | solution.py:231
  143.6 0.5 broadcast_xor_fusion._
  144.1 7.0 %shared.1 = bf16[4,2,6,32,128]{4,3,2,1,0:T(8,128)(2,1)} custom-call(s32[4]{0:T(128)} %broadcast_xor_fusion._, bf16[4,2,6,32,128]{4,3,2,1,0:T(8,128)(2,1)} %pad_maximum_fusion.x_ref, bf16[6144,128]{1,0:T(8,128)(2,1)} %g_ref.1, bf16[6144,128]{1,0:T(8,128)(2,1)} %u_ref.1, bf16[128,6144]{1,0:T(8,128)(2,1)} %d_ref.1), custom_call_target="tpu_custom_call" | custom-call | flops 150994944 | bytes 377487 | tf_op jit(solution)/shard_map/shared/pallas_call | solution.py:177
  151.1 11.1 %all-to-all-done.2 = bf16[4,6,240,128]{3,2,1,0:T(8,128)(2,1)S(1)} async-done(((bf16[4,6,240,128]{3,2,1,0:T(8,128)(2,1)}), bf16[4,6,240,128]{3,2,1,0:T(8,128)(2,1)S(1)}, u32[]{:S(2)}, u32[]{:S(2)}) %all-to-all-start.2) | async-done | bytes 1474592 | tf_op jit(solution)/shard_map/all_to_all | solution.py:231
  162.2 0.9 slice.37
  163.1 2.2 %collective-permute-start.10 = (bf16[2,2,6,32,128]{4,3,2,1,0:T(8,128)(2,1)S(1)}, bf16[2,2,6,32,128]{4,3,2,1,0:T(8,128)(2,1)S(1)}, u32[]{:S(2)}, u32[]{:S(2)}) collective-permute-start(bf16[2,2,6,32,128]{4,3,2,1,0:T(8,128)(2,1)S(1)} %slice.37), channel_id=1, source_target_pairs={{0,4},{4,0},{8,12},{12,8},{1,5},{5,1},{9,13},{13,9},{2,6},{6,2},{1... | collective-permute-start | bytes 589832 | tf_op jit(solution)/shard_map/ppermute | solution.py:221
  165.3 0.3 reduce_sum.32
  165.6 0.9 copy.33
  166.5 12.3 %all-to-all-start.3 = ((bf16[48,32,128]{2,1,0:T(8,128)(2,1)}), bf16[48,32,128]{2,1,0:T(8,128)(2,1)S(1)}, u32[]{:S(2)}, u32[]{:S(2)}) async-start(bf16[48,32,128]{2,1,0:T(8,128)(2,1)} %copy.33), calls=%async_computation.3 | async-start | bytes 786432 | tf_op jit(solution)/shard_map/all_to_all | solution.py:231
  178.9 3.7 %collective-permute-start.11 = (bf16[1,2,6,32,128]{4,3,2,1,0:T(8,128)(2,1)S(1)}, bf16[1,2,6,32,128]{4,3,2,1,0:T(8,128)(2,1)S(1)}, u32[]{:S(2)}, u32[]{:S(2)}) collective-permute-start(bf16[1,2,6,32,128]{4,3,2,1,0:T(8,128)(2,1)S(1)} %slice.46), channel_id=1, source_target_pairs={{0,8},{4,12},{8,0},{12,4},{1,9},{5,13},{9,1},{13,5},{2,10},{6,14},... | collective-permute-start | bytes 294920 | tf_op jit(solution)/shard_map/ppermute | solution.py:221
  182.6 3.1 %collective-permute-done.11 = bf16[1,2,6,32,128]{4,3,2,1,0:T(8,128)(2,1)S(1)} collective-permute-done((bf16[1,2,6,32,128]{4,3,2,1,0:T(8,128)(2,1)S(1)}, bf16[1,2,6,32,128]{4,3,2,1,0:T(8,128)(2,1)S(1)}, u32[]{:S(2)}, u32[]{:S(2)}) %collective-permute-start.11) | collective-permute-done | bytes 98336 | tf_op jit(solution)/shard_map/ppermute | solution.py:221
  185.8 2.3 %collective-permute-start.12 = (bf16[6,32,128]{2,1,0:T(8,128)(2,1)S(1)}, bf16[6,32,128]{2,1,0:T(8,128)(2,1)S(1)}, u32[]{:S(2)}, u32[]{:S(2)}) collective-permute-start(bf16[6,32,128]{2,1,0:T(8,128)(2,1)S(1)} %select_bitcast_fusion), channel_id=1, source_target_pairs={{0,2},{2,0},{1,3},{3,1},{4,6},{6,4},{5,7},{7,5},{8,10},{10,8},{9,1... | collective-permute-start | bytes 147464 | tf_op jit(solution)/shard_map/ppermute | solution.py:218
  188.2 0.4 copy.30
  188.7 3.3 %collective-permute-done.12 = bf16[6,32,128]{2,1,0:T(8,128)(2,1)S(1)} collective-permute-done((bf16[6,32,128]{2,1,0:T(8,128)(2,1)S(1)}, bf16[6,32,128]{2,1,0:T(8,128)(2,1)S(1)}, u32[]{:S(2)}, u32[]{:S(2)}) %collective-permute-start.12) | collective-permute-done | bytes 49184 | tf_op jit(solution)/shard_map/ppermute | solution.py:218
  192.1 5.2 %all-to-all-done.3 = bf16[48,32,128]{2,1,0:T(8,128)(2,1)S(1)} async-done(((bf16[48,32,128]{2,1,0:T(8,128)(2,1)}), bf16[48,32,128]{2,1,0:T(8,128)(2,1)S(1)}, u32[]{:S(2)}, u32[]{:S(2)}) %all-to-all-start.3) | async-done | bytes 393248 | tf_op jit(solution)/shard_map/all_to_all | solution.py:231
  197.3 0.7 fusion.8
  198.0 8.2 %collective-permute-start.13 = (f32[3,32,128]{2,1,0:T(8,128)S(1)}, f32[3,32,128]{2,1,0:T(8,128)S(1)}, u32[]{:S(2)}, u32[]{:S(2)}) collective-permute-start(f32[3,32,128]{2,1,0:T(8,128)S(1)} %slice_select_fusion), channel_id=1, source_target_pairs={{0,1},{1,0},{2,3},{3,2},{4,5},{5,4},{6,7},{7,6},{8,9},{9,8},{10,11... | collective-permute-start | bytes 147464 | tf_op jit(solution)/shard_map/ppermute | solution.py:303
  206.2 0.9 collective-permute-done.13
  207.0 0.6 copy_bitcast_fusion.1
  (40 shorter events, 1.3 us)
Async XLA Ops:
  20.0 45.8 %collective-permute-start.4 = (bf16[2,3072,128]{2,1,0:T(8,128)(2,1)}, bf16[2,3072,128]{2,1,0:T(8,128)(2,1)S(1)}, u32[]{:S(2)}, u32[]{:S(2)}) collective-permute-start(bf16[2,3072,128]{2,1,0:T(8,128)(2,1)} %get-tuple-element.35), channel_id=1, source_target_pairs={{0,2},{2,0},{1,3},{3,1},{4,6},{6,4},{5,7},{7,5},{8,10},{10,8},{9,1... | collective-permute-start | bytes 4718600 | tf_op jit(solution)/shard_map/ppermute | solution.py:218
  21.9 59.3 %collective-permute-start = (bf16[2,3072,128]{2,1,0:T(8,128)(2,1)}, bf16[2,3072,128]{2,1,0:T(8,128)(2,1)}, u32[]{:S(2)}, u32[]{:S(2)}) collective-permute-start(bf16[2,3072,128]{2,1,0:T(8,128)(2,1)} %get-tuple-element.31.refs_0_), channel_id=1, source_target_pairs={{0,1},{1,0},{2,3},{3,2},{4,5},{5,4},{6,7},{7,6},{8,9},{9,8},{10,11... | collective-permute-start | bytes 4718600 | tf_op jit(solution)/shard_map/ppermute | solution.py:224
  24.1 57.0 %all-to-all-start = ((bf16[48,32,128]{2,1,0:T(8,128)(2,1)}), bf16[48,32,128]{2,1,0:T(8,128)(2,1)S(1)}, u32[]{:S(2)}, u32[]{:S(2)}) async-start(bf16[48,32,128]{2,1,0:T(8,128)(2,1)} %bitcast.9), calls=%async_computation | async-start | bytes 786432 | tf_op jit(solution)/shard_map/all_to_all | solution.py:231
  36.7 44.4 %collective-permute-start.1 = (bf16[128,3072]{1,0:T(8,128)(2,1)}, bf16[128,3072]{1,0:T(8,128)(2,1)S(1)}, u32[]{:S(2)}, u32[]{:S(2)}) collective-permute-start(bf16[128,3072]{1,0:T(8,128)(2,1)} %get-tuple-element.32.refs_0_), channel_id=1, source_target_pairs={{0,1},{1,0},{2,3},{3,2},{4,5},{5,4},{6,7},{7,6},{8,9},{9,8},{10,11... | collective-permute-start | bytes 2359304 | tf_op jit(solution)/shard_map/ppermute | solution.py:224
  65.7 17.7 %copy-start.2 = (bf16[2,3072,128]{2,1,0:T(8,128)(2,1)}, bf16[2,3072,128]{2,1,0:T(8,128)(2,1)S(1)}, u32[]{:S(2)}) copy-start(bf16[2,3072,128]{2,1,0:T(8,128)(2,1)S(1)} %collective-permute-done.4.refs_2_) | copy-start | bytes 4718596
  65.7 45.4 %collective-permute-start.5 = (bf16[2,3072,128]{2,1,0:T(8,128)(2,1)S(1)}, bf16[2,3072,128]{2,1,0:T(8,128)(2,1)}, u32[]{:S(2)}, u32[]{:S(2)}) collective-permute-start(bf16[2,3072,128]{2,1,0:T(8,128)(2,1)S(1)} %collective-permute-done.4.refs_2_), channel_id=1, source_target_pairs={{0,1},{1,0},{2,3},{3,2},{4,5},{5,4},{6,7},{7,6},{8,9},{9,8},{10,11... | collective-permute-start | bytes 4718600 | tf_op jit(solution)/shard_map/ppermute | solution.py:224
  69.0 5.2 %collective-permute-start.2 = (bf16[6,32,128]{2,1,0:T(8,128)(2,1)S(1)}, bf16[6,32,128]{2,1,0:T(8,128)(2,1)S(1)}, u32[]{:S(2)}, u32[]{:S(2)}) collective-permute-start(bf16[6,32,128]{2,1,0:T(8,128)(2,1)S(1)} %get-tuple-element.33), channel_id=1, source_target_pairs={{0,2},{2,0},{1,3},{3,1},{4,6},{6,4},{5,7},{7,5},{8,10},{10,8},{9,1... | collective-permute-start | bytes 147464 | tf_op jit(solution)/shard_map/ppermute | solution.py:218
  74.2 6.9 %collective-permute-start.3 = (bf16[1,2,6,32,128]{4,3,2,1,0:T(8,128)(2,1)S(1)}, bf16[1,2,6,32,128]{4,3,2,1,0:T(8,128)(2,1)S(1)}, u32[]{:S(2)}, u32[]{:S(2)}) collective-permute-start(bf16[1,2,6,32,128]{4,3,2,1,0:T(8,128)(2,1)S(1)} %maximum_select_fusion), channel_id=1, source_target_pairs={{0,8},{4,12},{8,0},{12,4},{1,9},{5,13},{9,1},{13,5},{2,10},{6,14},... | collective-permute-start | bytes 294920 | tf_op jit(solution)/shard_map/ppermute | solution.py:221
  81.1 0.9 copy-start.3
  83.5 27.6 %all-to-all-start.1 = ((bf16[4,6,240,128]{3,2,1,0:T(8,128)(2,1)}), bf16[4,6,240,128]{3,2,1,0:T(8,128)(2,1)S(1)}, u32[]{:S(2)}, u32[]{:S(2)}) async-start(bf16[4,6,240,128]{3,2,1,0:T(8,128)(2,1)} %broadcast_in_dim.66), calls=%async_computation.1 | async-start | bytes 2949120 | tf_op jit(solution)/shard_map/all_to_all | solution.py:231
  87.0 19.3 %collective-permute-start.7 = (bf16[128,3072]{1,0:T(8,128)(2,1)}, bf16[128,3072]{1,0:T(8,128)(2,1)}, u32[]{:S(2)}, u32[]{:S(2)}) collective-permute-start(bf16[128,3072]{1,0:T(8,128)(2,1)} %get-tuple-element.41), channel_id=1, source_target_pairs={{0,2},{2,0},{1,3},{3,1},{4,6},{6,4},{5,7},{7,5},{8,10},{10,8},{9,1... | collective-permute-start | bytes 2359304 | tf_op jit(solution)/shard_map/ppermute | solution.py:218
  106.3 22.7 %collective-permute-start.8 = (bf16[128,3072]{1,0:T(8,128)(2,1)}, bf16[128,3072]{1,0:T(8,128)(2,1)}, u32[]{:S(2)}, u32[]{:S(2)}) collective-permute-start(bf16[128,3072]{1,0:T(8,128)(2,1)} %collective-permute-done.7.refs_2_), channel_id=1, source_target_pairs={{0,1},{1,0},{2,3},{3,2},{4,5},{5,4},{6,7},{7,6},{8,9},{9,8},{10,11... | collective-permute-start | bytes 2359304 | tf_op jit(solution)/shard_map/ppermute | solution.py:224
  111.1 1.1 copy-start
  118.3 14.9 %collective-permute-start.6 = (bf16[240,1024]{1,0:T(8,128)(2,1)}, bf16[240,1024]{1,0:T(8,128)(2,1)S(1)}, u32[]{:S(2)}, u32[]{:S(2)}) collective-permute-start(bf16[240,1024]{1,0:T(8,128)(2,1)} %get-tuple-element.40), channel_id=1, source_target_pairs={{0,2},{2,0},{1,3},{3,1},{4,6},{6,4},{5,7},{7,5},{8,10},{10,8},{9,1... | collective-permute-start | bytes 1474568 | tf_op jit(solution)/shard_map/ppermute | solution.py:218
  120.2 8.1 %collective-permute-start.9 = (bf16[2,2,6,32,128]{4,3,2,1,0:T(8,128)(2,1)S(1)}, bf16[2,2,6,32,128]{4,3,2,1,0:T(8,128)(2,1)S(1)}, u32[]{:S(2)}, u32[]{:S(2)}) collective-permute-start(bf16[2,2,6,32,128]{4,3,2,1,0:T(8,128)(2,1)S(1)} %pad_maximum_fusion.1), channel_id=1, source_target_pairs={{0,4},{4,0},{8,12},{12,8},{1,5},{5,1},{9,13},{13,9},{2,6},{6,2},{1... | collective-permute-start | bytes 589832 | tf_op jit(solution)/shard_map/ppermute | solution.py:221
  133.2 0.8 copy-start.4
  139.3 4.3 %copy-start.5 = (s32[4]{0:T(128)S(1)}, s32[4]{0:T(128)}, u32[]{:S(2)}) copy-start(s32[4]{0:T(128)} %constant.63.clone) | copy-start | bytes 52
  139.3 22.9 %all-to-all-start.2 = ((bf16[4,6,240,128]{3,2,1,0:T(8,128)(2,1)}), bf16[4,6,240,128]{3,2,1,0:T(8,128)(2,1)S(1)}, u32[]{:S(2)}, u32[]{:S(2)}) async-start(bf16[4,6,240,128]{3,2,1,0:T(8,128)(2,1)} %down.1), calls=%async_computation.2 | async-start | bytes 2949120 | tf_op jit(solution)/shard_map/all_to_all | solution.py:231
  163.1 15.6 %collective-permute-start.10 = (bf16[2,2,6,32,128]{4,3,2,1,0:T(8,128)(2,1)S(1)}, bf16[2,2,6,32,128]{4,3,2,1,0:T(8,128)(2,1)S(1)}, u32[]{:S(2)}, u32[]{:S(2)}) collective-permute-start(bf16[2,2,6,32,128]{4,3,2,1,0:T(8,128)(2,1)S(1)} %slice.37), channel_id=1, source_target_pairs={{0,4},{4,0},{8,12},{12,8},{1,5},{5,1},{9,13},{13,9},{2,6},{6,2},{1... | collective-permute-start | bytes 589832 | tf_op jit(solution)/shard_map/ppermute | solution.py:221
  165.6 13.2 %copy-start.1 = (bf16[4,2,6,32,128]{4,3,2,1,0:T(8,128)(2,1)S(1)}, bf16[4,2,6,32,128]{4,3,2,1,0:T(8,128)(2,1)}, u32[]{:S(2)}) copy-start(bf16[4,2,6,32,128]{4,3,2,1,0:T(8,128)(2,1)} %shared.1) | copy-start | bytes 1179652
  166.5 30.8 %all-to-all-start.3 = ((bf16[48,32,128]{2,1,0:T(8,128)(2,1)}), bf16[48,32,128]{2,1,0:T(8,128)(2,1)S(1)}, u32[]{:S(2)}, u32[]{:S(2)}) async-start(bf16[48,32,128]{2,1,0:T(8,128)(2,1)} %copy.33), calls=%async_computation.3 | async-start | bytes 786432 | tf_op jit(solution)/shard_map/all_to_all | solution.py:231
  178.9 6.9 %collective-permute-start.11 = (bf16[1,2,6,32,128]{4,3,2,1,0:T(8,128)(2,1)S(1)}, bf16[1,2,6,32,128]{4,3,2,1,0:T(8,128)(2,1)S(1)}, u32[]{:S(2)}, u32[]{:S(2)}) collective-permute-start(bf16[1,2,6,32,128]{4,3,2,1,0:T(8,128)(2,1)S(1)} %slice.46), channel_id=1, source_target_pairs={{0,8},{4,12},{8,0},{12,4},{1,9},{5,13},{9,1},{13,5},{2,10},{6,14},... | collective-permute-start | bytes 294920 | tf_op jit(solution)/shard_map/ppermute | solution.py:221
  185.8 6.3 %collective-permute-start.12 = (bf16[6,32,128]{2,1,0:T(8,128)(2,1)S(1)}, bf16[6,32,128]{2,1,0:T(8,128)(2,1)S(1)}, u32[]{:S(2)}, u32[]{:S(2)}) collective-permute-start(bf16[6,32,128]{2,1,0:T(8,128)(2,1)S(1)} %select_bitcast_fusion), channel_id=1, source_target_pairs={{0,2},{2,0},{1,3},{3,1},{4,6},{6,4},{5,7},{7,5},{8,10},{10,8},{9,1... | collective-permute-start | bytes 147464 | tf_op jit(solution)/shard_map/ppermute | solution.py:218
  198.0 9.0 %collective-permute-start.13 = (f32[3,32,128]{2,1,0:T(8,128)S(1)}, f32[3,32,128]{2,1,0:T(8,128)S(1)}, u32[]{:S(2)}, u32[]{:S(2)}) collective-permute-start(f32[3,32,128]{2,1,0:T(8,128)S(1)} %slice_select_fusion), channel_id=1, source_target_pairs={{0,1},{1,0},{2,3},{3,2},{4,5},{5,4},{6,7},{7,6},{8,9},{9,8},{10,11... | collective-permute-start | bytes 147464 | tf_op jit(solution)/shard_map/ppermute | solution.py:303

commit v3 on v2

--- a/solution.py
+++ b/solution.py
@@ -8,6 +8,7 @@
 
 
 LANES = 128
+SMALL = pltpu.CompilerParams(dimension_semantics=("arbitrary",), vmem_limit_bytes=24 * 1024 * 1024)
 PARAMS = pltpu.CompilerParams(dimension_semantics=("arbitrary",), vmem_limit_bytes=60 * 1024 * 1024)
 
 
@@ -32,45 +33,79 @@
     return pl.CostEstimate(flops=flops, bytes_accessed=flops // 400, transcendentals=0)
 
 
-def split_weights(y, w_gate, w_up, w_down, count, width):
-    hidden = w_gate.shape[1]
-
-    def body(_, gm, go, um, uo, dm, do, mine, other, mine_down, other_down):
-        mine[0] = gm[...]
-        mine[1] = um[...]
-        other[0] = go[...]
-        other[1] = uo[...]
-        mine_down[...] = dm[...]
-        other_down[...] = do[...]
-
-    near = pl.BlockSpec((width, hidden), lambda i, y: (2 * i + y[0], 0))
-    far = pl.BlockSpec((width, hidden), lambda i, y: (2 * i + 1 - y[0], 0))
-    near_down = pl.BlockSpec((hidden, width), lambda i, y: (0, 2 * i + y[0]))
-    far_down = pl.BlockSpec((hidden, width), lambda i, y: (0, 2 * i + 1 - y[0]))
-    pair = pl.BlockSpec((2, width, hidden), lambda i, y: (0, i, 0))
-    column = pl.BlockSpec((hidden, width), lambda i, y: (0, i))
-    pair_shape = jax.ShapeDtypeStruct((2, count * width, hidden), w_gate.dtype)
-    column_shape = jax.ShapeDtypeStruct((hidden, count * width), w_gate.dtype)
+def copies_call(body, y, arrays, shapes, stages):
+    scratch = [pltpu.VMEM(s, jnp.bfloat16) for s in stages]
     return pl.pallas_call(
         body,
-        grid_spec=pltpu.PrefetchScalarGridSpec(
-            num_scalar_prefetch=1,
-            grid=(count,),
-            in_specs=[near, far, near, far, near_down, far_down],
-            out_specs=[pair, pair, column, column],
-        ),
-        out_shape=[pair_shape, pair_shape, column_shape, column_shape],
+        in_specs=[pl.BlockSpec(memory_space=pltpu.SMEM)] + [pl.BlockSpec(memory_space=pl.ANY)] * len(arrays),
+        out_specs=[pl.BlockSpec(memory_space=pl.ANY)] * len(shapes),
+        out_shape=[jax.ShapeDtypeStruct(s, jnp.bfloat16) for s in shapes],
+        scratch_shapes=[*scratch, pltpu.SemaphoreType.DMA((2, len(stages)))],
         cost_estimate=estimate(10**9),
-        compiler_params=PARAMS,
-        name="split",
-    )(y[None], w_gate, w_gate, w_up, w_up, w_down, w_down)
-
-
-def partial_sums(x, ins):
+        compiler_params=pltpu.CompilerParams(vmem_limit_bytes=60 * 1024 * 1024),
+    )(y[None], *arrays)
+
+
+def run_copies(pairs, stages, sems):
+    first = [pltpu.make_async_copy(src, stage, sems.at[0, n]) for n, ((src, _), stage) in enumerate(zip(pairs, stages))]
+    second = [pltpu.make_async_copy(stage, dst, sems.at[1, n]) for n, ((_, dst), stage) in enumerate(zip(pairs, stages))]
+    for copy in first:
+        copy.start()
+    for one, two in zip(first, second):
+        one.wait()
+        two.start()
+    for copy in second:
+        copy.wait()
+
+
+def blocks_of(y, w, out, at, count, width):
+    pairs = []
+    for x in range(count):
+        rows = pl.ds(pl.multiple_of((2 * x + y) * width, width), width)
+        pairs.append((w.at[rows, :], out.at[pl.ds(at + x * width, width), :]))
+    return pairs
+
+
+def columns_of(y, w, out, count, width):
+    pairs = []
+    for x in range(count):
+        lanes = pl.ds(pl.multiple_of((2 * x + y) * width, width), width)
+        pairs.append((w.at[:, lanes], out.at[:, pl.ds(x * width, width)]))
+    return pairs
+
+
+def rows_for_neighbour(y, w_gate, w_up, lines, count, width):
+    def body(y_ref, g, u, t, first, second, *rest):
+        other = 1 - y_ref[0]
+        pairs = [(t, first.at[pl.ds(count * width, lines.shape[0]), :])]
+        pairs += blocks_of(other, g, first, 0, count, width) + blocks_of(other, u, second, 0, count, width)
+        run_copies(pairs, rest[:-1], rest[-1])
+
+    hidden = w_gate.shape[1]
+    shapes = [(count * width + lines.shape[0], hidden), (count * width, hidden)]
+    stages = [lines.shape] + [(width, hidden)] * (2 * count)
+    return copies_call(body, y, (w_gate, w_up, lines), shapes, stages)
+
+
+def own_blocks(y, w_gate, w_up, w_down, count, width):
+    def body(y_ref, g, u, d, out, near, far, *rest):
+        y = y_ref[0]
+        pairs = blocks_of(y, g, out, 0, count, width) + blocks_of(y, u, out, count * width, count, width)
+        pairs += columns_of(y, d, near, count, width) + columns_of(1 - y, d, far, count, width)
+        run_copies(pairs, rest[:-1], rest[-1])
+
+    hidden = w_gate.shape[1]
+    shapes = [(2 * count * width, hidden), (hidden, count * width), (hidden, count * width)]
+    stages = [(width, hidden)] * (2 * count) + [(hidden, width)] * (2 * count)
+    return copies_call(body, y, (w_gate, w_up, w_down), shapes, stages)
+
+
+def partial_sums(x, gates, ups):
     chips, chunks, rows, _ = x.shape
-    hidden = ins[0].shape[2]
+    ins = (*gates, *ups)
+    hidden = ins[0].shape[1]
     width = chunks * LANES
-    wide = 2 * len(ins) * hidden
+    wide = len(ins) * hidden
 
     def body(x_ref, *refs):
         w, acc, sent = refs[: len(ins)], refs[-2], refs[-1]
@@ -81,7 +116,7 @@
             acc[...] = jnp.zeros_like(acc)
 
         lines = jnp.concatenate([x_ref[0, j] for j in range(chunks)], axis=1)
-        weights = jnp.concatenate([r[k] for k in range(2) for r in w], axis=1)
+        weights = jnp.concatenate([r[...] for r in w], axis=1)
         acc[...] += jnp.dot(lines, weights, preferred_element_type=jnp.float32)
 
         @pl.when(i == chips - 1)
@@ -93,7 +128,9 @@
         body,
         grid=(chips,),
         in_specs=[pl.BlockSpec((1, chunks, rows, LANES), lambda i: (i, 0, 0, 0))]
-        + [pl.BlockSpec((2, width, hidden), lambda i: (0, i, 0))] * len(ins),
+        + [pl.BlockSpec((width, hidden), lambda i: (i, 0))] * len(gates)
+        + [pl.BlockSpec((width, hidden), lambda i: (chips + i, 0))] * 2
+        + [pl.BlockSpec((width, hidden), lambda i: (i, 0))] * 2,
         out_specs=[whole, whole],
         out_shape=[
             jax.ShapeDtypeStruct((rows, wide), jnp.float32),
@@ -135,28 +172,36 @@
         out_shape=jax.ShapeDtypeStruct((count, chunks, rows, LANES), jnp.bfloat16),
         scratch_shapes=[pltpu.VMEM((rows, wide // 2), jnp.bfloat16)],
         cost_estimate=estimate(2 * rows * count * width * 4 * part),
-        compiler_params=PARAMS,
+        compiler_params=SMALL,
         name="down",
     )(sums, other, *outs)
 
 
-def shared_expert(x, at, w_gate, w_up, w_down):
-    pairs, ys, chunks, rows, _ = x.shape
+def shared_expert(x, rest, at, w_gate, w_up, w_down):
+    half, ys, chunks, rows, _ = x.shape
+    pairs = 2 * half
     hidden = w_gate.shape[1]
     width = ys * chunks * LANES
 
-    def body(_, x_ref, g_ref, u_ref, d_ref, out, acc, h):
+    def body(_, x_ref, r_ref, g_ref, u_ref, d_ref, out, acc, h):
         i = pl.program_id(0)
 
         @pl.when(i == 0)
         def _():
             acc[...] = jnp.zeros_like(acc)
 
-        @pl.when(i < pairs)
-        def _():
-            lines = jnp.concatenate([x_ref[0, y, j] for y in range(ys) for j in range(chunks)], axis=1)
+        def add(ref):
+            lines = jnp.concatenate([ref[0, y, j] for y in range(ys) for j in range(chunks)], axis=1)
             weights = jnp.concatenate([g_ref[...], u_ref[...]], axis=1)
             acc[...] += jnp.dot(lines, weights, preferred_element_type=jnp.float32)
+
+        @pl.when(i < half)
+        def _():
+            add(x_ref)
+
+        @pl.when((i >= half) & (i < pairs))
+        def _():
+            add(r_ref)
 
         @pl.when(i == pairs)
         def _():
@@ -180,7 +225,8 @@
             num_scalar_prefetch=1,
             grid=(2 * pairs,),
             in_specs=[
-                pl.BlockSpec(block, lambda i, at: (first(i), 0, 0, 0, 0)),
+                pl.BlockSpec(block, lambda i, at: (jnp.minimum(i, half - 1), 0, 0, 0, 0)),
+                pl.BlockSpec(block, lambda i, at: (jnp.clip(i - half, 0, half - 1), 0, 0, 0, 0)),
                 w_in,
                 w_in,
                 pl.BlockSpec((hidden, width), lambda i, at: (0, at[second(i)])),
@@ -188,11 +234,11 @@
             out_specs=pl.BlockSpec(block, lambda i, at: (second(i), 0, 0, 0, 0)),
             scratch_shapes=[pltpu.VMEM((rows, 2 * hidden), jnp.float32), pltpu.VMEM((rows, hidden), jnp.bfloat16)],
         ),
-        out_shape=jax.ShapeDtypeStruct(x.shape, jnp.bfloat16),
+        out_shape=jax.ShapeDtypeStruct((pairs, *x.shape[1:]), jnp.bfloat16),
         cost_estimate=estimate(6 * rows * pairs * width * hidden),
         compiler_params=PARAMS,
         name="shared",
-    )(at, x, w_gate, w_up, w_down)
+    )(at, x, rest, w_gate, w_up, w_down)
 
 
 def local(
@@ -248,40 +294,45 @@
     select = match.astype(jnp.bfloat16).reshape(experts * message, columns)
     buckets = jnp.dot(select, stacked.reshape(columns, LANES), preferred_element_type=jnp.float32)
     buckets = buckets.astype(jnp.bfloat16).reshape(experts, message, LANES)
+    w_gate, w_up, w_down = routed_gate[0], routed_up[0], routed_down[0]
     received = exchange(buckets, "ep")
-
-    _, w_gate, w_up, w_down, ours = lax.optimization_barrier(
-        (buckets, routed_gate[0], routed_up[0], routed_down[0], stacked)
-    )
-    theirs = to_y(ours)
-    mine, other, mine_down, other_down = split_weights(yi, w_gate, w_up, w_down, xs, width)
+    _, w_gate, w_up, w_down, lines = lax.optimization_barrier(
+        (buckets, w_gate, w_up, w_down, stacked.reshape(columns, LANES))
+    )
+    other, other_up = rows_for_neighbour(yi, w_gate, w_up, lines, xs, width)
     got = to_y(other)
+    got_up = to_y(other_up)
+    mine, mine_down, other_down = own_blocks(yi, w_gate, w_up, w_down, xs, width)
     partner = to_c(mine)
     partner_down = to_c(mine_down)
-    whole = jnp.where(yi == 0, jnp.stack([ours, theirs]), jnp.stack([theirs, ours]))[None]
-    whole = jnp.concatenate([whole, to_x(whole, 2)], axis=0)
-    received, partner, partner_down, whole = lax.optimization_barrier(
-        (received, partner, partner_down, whole)
-    )
+    received, partner, partner_down = lax.optimization_barrier((received, partner, partner_down))
     rows = jnp.swapaxes(received, 0, 1)[:used].reshape(chunks, routed_rows, LANES)
     gathered = exchange(jnp.broadcast_to(rows[None], (xs,) + rows.shape), "x")
     got_down = to_y(other_down)
     partner_got = to_c(got)
-    gathered, partner_got = lax.optimization_barrier((gathered, partner_got))
-    sums, sent = partial_sums(gathered, (mine, partner, got, partner_got))
+    theirs = got[xs * width :].reshape(stacked.shape)
+    whole = jnp.where(yi == 0, jnp.stack([stacked, theirs]), jnp.stack([theirs, stacked]))[None]
+    whole_x = to_x(whole, 2)
+    partner_got_up = to_c(got_up)
+    gathered, partner_got, partner_got_up = lax.optimization_barrier((gathered, partner_got, partner_got_up))
+    sums, sent = partial_sums(
+        gathered, (mine, partner, got, partner_got), (mine, partner, got_up, partner_got_up)
+    )
     other_sums = to_y(sent)
-    whole = jnp.concatenate([whole, to_x(whole, 1)], axis=0)
+    whole = jnp.concatenate([whole, whole_x], axis=0)
+    rest = to_x(whole, 1)
     partner_got_down = to_c(got_down)
-    other_sums, partner_got_down, whole = lax.optimization_barrier((other_sums, partner_got_down, whole))
+    other_sums, partner_got_down, rest = lax.optimization_barrier((other_sums, partner_got_down, rest))
     products = down(sums, other_sums, (mine_down, partner_down, got_down, partner_got_down), xs, chunks)
     reduced = exchange(products, "x")
     at = jnp.bitwise_xor(jnp.array([0, 2, 1, 3], jnp.int32), xi)
-    part = shared_expert(whole, at, shared_gate, shared_up, shared_down)
+    part = shared_expert(whole, rest, at, shared_gate, shared_up, shared_down)
+    far = to_x(part[2:], 1)
     reduced, part = lax.optimization_barrier((reduced, part))
     total = jnp.sum(reduced.astype(jnp.float32), axis=0).astype(jnp.bfloat16)
     outcome = jnp.pad(total.reshape(used, experts, LANES), ((0, message - used), (0, 0), (0, 0)))
     returned = exchange(jnp.swapaxes(outcome, 0, 1), "ep")
-    part = halve(part, 1)
+    part = (part[:2].astype(jnp.float32) + far.astype(jnp.float32)).astype(part.dtype)
     part = halve(part, 2)[0]
     kept = jnp.where(yi == 0, part[0], part[1])
     lost = jnp.where(yi == 0, part[1], part[0])

time: 209 us -> 196 us (0.938)
  waiting for transfers between devices: 84.8 us -> 65.8 us
  starting transfers between devices: 74.4 us -> 82.2 us
    ppermute x5, waiting for transfers between devices: 54.9 us -> 32.8 us  [to_y(): return lax.ppermute(v, 'y', swap)]
    all_to_all x4, waiting for transfers between devices: 16.3 us -> 20.7 us  [exchange(): return lax.all_to_all(v, axes, split_axis=0, concat_axis=0, tiled=True)]
    ppermute x5, starting transfers between devices: 9.92 us -> 13.2 us  [to_y(): return lax.ppermute(v, 'y', swap)]
    pallas_call x1, Pallas kernels: 5.29 us -> 2.92 us  [down(): pl.pallas_call(body, grid=(count,), in_specs=[whole, whole] + [pl.BlockSp...]
    ppermute x4, starting transfers between devices: 11.1 us -> 13.4 us  [to_x(): return lax.ppermute(v, 'x', [(i, i ^ bit) for i in range(xs)])]
    ppermute x4 -> x5, starting transfers between devices: 12.5 us -> 13.1 us  [to_c(): return lax.ppermute(v, 'c', swap)]
    pallas_call x1 -> x2, Pallas kernels: 5.13 us -> 5.57 us  [copies_call(): pl.pallas_call(body, in_specs=[pl.BlockSpec(memory_space=pltpu.SMEM)] + [...]
  transfers between devices with their start and end apart: 18 -> 19, of which waited for: 11 -> 11; matrix products, arithmetic and copies ran while one was open for 2% -> 3% of each run, Pallas kernels for 6% -> 8%
where the time goes in v3:
time: 196 us; the launch traced here: 194 us
  starting transfers between devices  82.2 us (42%)
  waiting for transfers between devices  65.8 us (34%)
  Pallas kernels  21.9 us (11%)
  blocking collectives  12.2 us (6%)
  local copies, waits for them, and re-layouts  6.85 us (3%)
  other arithmetic  2.93 us (1%)
  matrix products  1.99 us (1%)
    ppermute x5, waiting for transfers between devices, to_y(): return lax.ppermute(v, 'y', swap)  32.8 us
    all_to_all x4, starting transfers between devices, exchange(): return lax.all_to_all(v, axes, split_axis=0, concat_axis=0, tiled=True)  32.3 us
    all_to_all x4, waiting for transfers between devices, exchange(): return lax.all_to_all(v, axes, split_axis=0, concat_axis=0, tiled=True)  20.7 us
    ppermute x4, starting transfers between devices, to_x(): return lax.ppermute(v, 'x', [(i, i ^ bit) for i in range(xs)])  13.4 us
    ppermute x5, starting transfers between devices, to_y(): return lax.ppermute(v, 'y', swap)  13.2 us
    ppermute x5, starting transfers between devices, to_c(): return lax.ppermute(v, 'c', swap)  13.1 us
    all_gather x1, blocking collectives, local(): pair = lax.all_gather(tokens, 'c', axis=1, tiled=True)  12.2 us
    ppermute x4, waiting for transfers between devices, to_x(): return lax.ppermute(v, 'x', [(i, i ^ bit) for i in range(xs)])  11.4 us
  transfers between devices with their start and end apart: 19, of which 11 were waited for; matrix products, arithmetic and copies ran while one was open for 3% of the time, Pallas kernels for 8%

profile of v3, /device:TPU:1, one launch (start us, length us, event | category | flops | bytes accessed | tf_op | source)
XLA Modules:
  0.0 194.3 jit_solution(11209747356450389867)
XLA Ops:
  0.2 12.2 %all_gather.3 = bf16[32,768]{1,0:T(8,128)(2,1)S(1)} all-gather(bf16[32,384]{1,0:T(8,128)(2,1)} %param.10), channel_id=1, replica_groups=mesh['ep'=48,'x'=4,'y'=2,'c'=2] {'c'}, dimensions={1}, use_global_device_ids=true | all-gather | bytes 73728 | tf_op jit(solution)/shard_map/all_gather | solution.py:286
  12.4 0.9 convert_reduce_fusion
  13.7 1.2 convolution_convert_fusion
  14.9 3.2 %shard_map.100 = (bf16[6144,128]{1,0:T(8,128)(2,1)}, bf16[128,3072]{1,0:T(8,128)(2,1)}, bf16[128,3072]{1,0:T(8,128)(2,1)}) custom-call(s32[1]{0:T(128)} %bitcast.10.y_ref, bf16[6144,128]{1,0:T(8,128)(2,1)} %bitcast.56, bf16[6144,128]{1,0:T(8,128)(2,1)} %bitcast.58, bf16[128,6144]{1,0:T(8,128)(2,1)} %bitcast.55), custom_call_target="tpu_custom_call" | custom-call | flops 1000000000 | bytes 2500000 | tf_op jit(solution)/shard_map/pallas_call | solution.py:38
  18.1 2.3 %collective-permute-start = (bf16[6144,128]{1,0:T(8,128)(2,1)}, bf16[6144,128]{1,0:T(8,128)(2,1)S(1)}, u32[]{:S(2)}, u32[]{:S(2)}) collective-permute-start(bf16[6144,128]{1,0:T(8,128)(2,1)} %get-tuple-element.32.refs_0_.refs_4_), channel_id=1, source_target_pairs={{0,1},{1,0},{2,3},{3,2},{4,5},{5,4},{6,7},{7,6},{8,9},{9,8},{10,11... | collective-permute-start | bytes 4718600 | tf_op jit(solution)/shard_map/ppermute | solution.py:270
  20.4 11.8 %all-to-all-start = ((bf16[48,32,128]{2,1,0:T(8,128)(2,1)}), bf16[48,32,128]{2,1,0:T(8,128)(2,1)S(1)}, u32[]{:S(2)}, u32[]{:S(2)}) async-start(bf16[48,32,128]{2,1,0:T(8,128)(2,1)} %bitcast.9), calls=%async_computation | async-start | bytes 786432 | tf_op jit(solution)/shard_map/all_to_all | solution.py:277
  32.2 2.4 %collective-permute-start.1 = (bf16[128,3072]{1,0:T(8,128)(2,1)}, bf16[128,3072]{1,0:T(8,128)(2,1)S(1)}, u32[]{:S(2)}, u32[]{:S(2)}) collective-permute-start(bf16[128,3072]{1,0:T(8,128)(2,1)} %get-tuple-element.33.refs_0_), channel_id=1, source_target_pairs={{0,1},{1,0},{2,3},{3,2},{4,5},{5,4},{6,7},{7,6},{8,9},{9,8},{10,11... | collective-permute-start | bytes 2359304 | tf_op jit(solution)/shard_map/ppermute | solution.py:270
  34.6 2.3 %shard_map.101 = (bf16[3264,128]{1,0:T(8,128)(2,1)}, bf16[3072,128]{1,0:T(8,128)(2,1)}) custom-call(s32[1]{0:T(128)} %bitcast.10.y_ref, bf16[6144,128]{1,0:T(8,128)(2,1)} %bitcast.57, bf16[6144,128]{1,0:T(8,128)(2,1)} %bitcast.59, bf16[192,128]{1,0:T(8,128)(2,1)} %bitcast.67), custom_call_target="tpu_custom_call" | custom-call | flops 1000000000 | bytes 2500000 | tf_op jit(solution)/shard_map/pallas_call | solution.py:38
  36.9 2.3 %collective-permute-start.2 = (bf16[3264,128]{1,0:T(8,128)(2,1)}, bf16[3264,128]{1,0:T(8,128)(2,1)}, u32[]{:S(2)}, u32[]{:S(2)}) collective-permute-start(bf16[3264,128]{1,0:T(8,128)(2,1)} %get-tuple-element.36), channel_id=1, source_target_pairs={{0,2},{2,0},{1,3},{3,1},{4,6},{6,4},{5,7},{7,5},{8,10},{10,8},{9,1... | collective-permute-start | bytes 2506760 | tf_op jit(solution)/shard_map/ppermute | solution.py:264
  39.3 3.0 %collective-permute-start.4 = (bf16[3072,128]{1,0:T(8,128)(2,1)}, bf16[3072,128]{1,0:T(8,128)(2,1)}, u32[]{:S(2)}, u32[]{:S(2)}) collective-permute-start(bf16[3072,128]{1,0:T(8,128)(2,1)} %get-tuple-element.37), channel_id=1, source_target_pairs={{0,2},{2,0},{1,3},{3,1},{4,6},{6,4},{5,7},{7,5},{8,10},{10,8},{9,1... | collective-permute-start | bytes 2359304 | tf_op jit(solution)/shard_map/ppermute | solution.py:264
  42.3 10.8 %all-to-all-done = bf16[48,32,128]{2,1,0:T(8,128)(2,1)S(1)} async-done(((bf16[48,32,128]{2,1,0:T(8,128)(2,1)}), bf16[48,32,128]{2,1,0:T(8,128)(2,1)S(1)}, u32[]{:S(2)}, u32[]{:S(2)}) %all-to-all-start) | async-done | bytes 393248 | tf_op jit(solution)/shard_map/all_to_all | solution.py:277
  53.2 1.5 broadcast_in_dim.67
  54.7 4.5 %all-to-all-start.1 = ((bf16[4,6,240,128]{3,2,1,0:T(8,128)(2,1)}), bf16[4,6,240,128]{3,2,1,0:T(8,128)(2,1)}, u32[]{:S(2)}, u32[]{:S(2)}) async-start(bf16[4,6,240,128]{3,2,1,0:T(8,128)(2,1)} %broadcast_in_dim.67), calls=%async_computation.1 | async-start | bytes 2949120 | tf_op jit(solution)/shard_map/all_to_all | solution.py:277
  59.2 2.3 %collective-permute-start.7 = (bf16[128,3072]{1,0:T(8,128)(2,1)S(1)}, bf16[128,3072]{1,0:T(8,128)(2,1)S(1)}, u32[]{:S(2)}, u32[]{:S(2)}) collective-permute-start(bf16[128,3072]{1,0:T(8,128)(2,1)S(1)} %copy-done.7), channel_id=1, source_target_pairs={{0,2},{2,0},{1,3},{3,1},{4,6},{6,4},{5,7},{7,5},{8,10},{10,8},{9,1... | collective-permute-start | bytes 2359304 | tf_op jit(solution)/shard_map/ppermute | solution.py:264
  61.5 2.4 %collective-permute-done.2.refs_2_ = bf16[3264,128]{1,0:T(8,128)(2,1)} collective-permute-done((bf16[3264,128]{1,0:T(8,128)(2,1)}, bf16[3264,128]{1,0:T(8,128)(2,1)}, u32[]{:S(2)}, u32[]{:S(2)}) %collective-permute-start.2) | collective-permute-done | bytes 835616 | tf_op jit(solution)/shard_map/ppermute | solution.py:264
  63.9 3.5 %collective-permute-start.3 = (bf16[3264,128]{1,0:T(8,128)(2,1)}, bf16[3264,128]{1,0:T(8,128)(2,1)}, u32[]{:S(2)}, u32[]{:S(2)}) collective-permute-start(bf16[3264,128]{1,0:T(8,128)(2,1)} %collective-permute-done.2.refs_2_), channel_id=1, source_target_pairs={{0,1},{1,0},{2,3},{3,2},{4,5},{5,4},{6,7},{7,6},{8,9},{9,8},{10,11... | collective-permute-start | bytes 2506760 | tf_op jit(solution)/shard_map/ppermute | solution.py:270
  67.4 13.4 %collective-permute-done.4.refs_6_ = bf16[3072,128]{1,0:T(8,128)(2,1)} collective-permute-done((bf16[3072,128]{1,0:T(8,128)(2,1)}, bf16[3072,128]{1,0:T(8,128)(2,1)}, u32[]{:S(2)}, u32[]{:S(2)}) %collective-permute-start.4) | collective-permute-done | bytes 786464 | tf_op jit(solution)/shard_map/ppermute | solution.py:264
  80.8 2.6 %collective-permute-start.5 = (bf16[3072,128]{1,0:T(8,128)(2,1)}, bf16[3072,128]{1,0:T(8,128)(2,1)}, u32[]{:S(2)}, u32[]{:S(2)}) collective-permute-start(bf16[3072,128]{1,0:T(8,128)(2,1)} %collective-permute-done.4.refs_6_), channel_id=1, source_target_pairs={{0,1},{1,0},{2,3},{3,2},{4,5},{5,4},{6,7},{7,6},{8,9},{9,8},{10,11... | collective-permute-start | bytes 2359304 | tf_op jit(solution)/shard_map/ppermute | solution.py:270
  83.4 14.2 %collective-permute-done.7.refs_2_ = bf16[128,3072]{1,0:T(8,128)(2,1)S(1)} collective-permute-done((bf16[128,3072]{1,0:T(8,128)(2,1)S(1)}, bf16[128,3072]{1,0:T(8,128)(2,1)S(1)}, u32[]{:S(2)}, u32[]{:S(2)}) %collective-permute-start.7) | collective-permute-done | bytes 786464 | tf_op jit(solution)/shard_map/ppermute | solution.py:264
  97.5 2.4 %collective-permute-start.8 = (bf16[128,3072]{1,0:T(8,128)(2,1)S(1)}, bf16[128,3072]{1,0:T(8,128)(2,1)S(1)}, u32[]{:S(2)}, u32[]{:S(2)}) collective-permute-start(bf16[128,3072]{1,0:T(8,128)(2,1)S(1)} %collective-permute-done.7.refs_2_), channel_id=1, source_target_pairs={{0,1},{1,0},{2,3},{3,2},{4,5},{5,4},{6,7},{7,6},{8,9},{9,8},{10,11... | collective-permute-start | bytes 2359304 | tf_op jit(solution)/shard_map/ppermute | solution.py:270
  100.0 0.8 slice.49
  100.8 6.3 %partial.1 = (f32[240,1024]{1,0:T(8,128)}, bf16[240,1024]{1,0:T(8,128)(2,1)}) custom-call(bf16[4,6,240,128]{3,2,1,0:T(8,128)(2,1)} %all-to-all-done.1.x_ref, bf16[6144,128]{1,0:T(8,128)(2,1)} %get-tuple-element.32.refs_0_.refs_4_, bf16[6144,128]{1,0:T(8,128)(2,1)} %copy-done.2, bf16[3264,128]{1,0:T(8,128)(2,1)} %collective-permute-done.2.refs_2_, ...), custom_call_target="tpu_custom_call" | custom-call | flops 1509949440 | bytes 3774873 | tf_op jit(solution)/shard_map/partial/pallas_call | solution.py:127
  107.1 2.8 %collective-permute-start.6 = (bf16[240,1024]{1,0:T(8,128)(2,1)}, bf16[240,1024]{1,0:T(8,128)(2,1)S(1)}, u32[]{:S(2)}, u32[]{:S(2)}) collective-permute-start(bf16[240,1024]{1,0:T(8,128)(2,1)} %get-tuple-element.43), channel_id=1, source_target_pairs={{0,2},{2,0},{1,3},{3,1},{4,6},{6,4},{5,7},{7,5},{8,10},{10,8},{9,1... | collective-permute-start | bytes 1474568 | tf_op jit(solution)/shard_map/ppermute | solution.py:264
  109.9 4.7 %collective-permute-start.9 = (bf16[1,2,6,32,128]{4,3,2,1,0:T(8,128)(2,1)S(1)}, bf16[1,2,6,32,128]{4,3,2,1,0:T(8,128)(2,1)S(1)}, u32[]{:S(2)}, u32[]{:S(2)}) collective-permute-start(bf16[1,2,6,32,128]{4,3,2,1,0:T(8,128)(2,1)S(1)} %maximum_select_fusion), channel_id=1, source_target_pairs={{0,8},{4,12},{8,0},{12,4},{1,9},{5,13},{9,1},{13,5},{2,10},{6,14},... | collective-permute-start | bytes 294920 | tf_op jit(solution)/shard_map/ppermute | solution.py:267
  114.5 2.8 %collective-permute-done.9 = bf16[1,2,6,32,128]{4,3,2,1,0:T(8,128)(2,1)S(1)} collective-permute-done((bf16[1,2,6,32,128]{4,3,2,1,0:T(8,128)(2,1)S(1)}, bf16[1,2,6,32,128]{4,3,2,1,0:T(8,128)(2,1)S(1)}, u32[]{:S(2)}, u32[]{:S(2)}) %collective-permute-start.9) | collective-permute-done | bytes 98336 | tf_op jit(solution)/shard_map/ppermute | solution.py:267
  117.3 3.1 %collective-permute-start.10 = (bf16[2,2,6,32,128]{4,3,2,1,0:T(8,128)(2,1)S(1)}, bf16[2,2,6,32,128]{4,3,2,1,0:T(8,128)(2,1)S(1)}, u32[]{:S(2)}, u32[]{:S(2)}) collective-permute-start(bf16[2,2,6,32,128]{4,3,2,1,0:T(8,128)(2,1)S(1)} %pad_maximum_fusion.x_ref), channel_id=1, source_target_pairs={{0,4},{4,0},{8,12},{12,8},{1,5},{5,1},{9,13},{13,9},{2,6},{6,2},{1... | collective-permute-start | bytes 589832 | tf_op jit(solution)/shard_map/ppermute | solution.py:267
  120.5 4.1 %collective-permute-done.10.r_ref = bf16[2,2,6,32,128]{4,3,2,1,0:T(8,128)(2,1)S(1)} collective-permute-done((bf16[2,2,6,32,128]{4,3,2,1,0:T(8,128)(2,1)S(1)}, bf16[2,2,6,32,128]{4,3,2,1,0:T(8,128)(2,1)S(1)}, u32[]{:S(2)}, u32[]{:S(2)}) %collective-permute-start.10) | collective-permute-done | bytes 196640 | tf_op jit(solution)/shard_map/ppermute | solution.py:267
  124.6 0.7 copy-done.5
  125.2 1.2 copy-done
  126.4 2.9 %down.1 = bf16[4,6,240,128]{3,2,1,0:T(8,128)(2,1)} custom-call(f32[240,1024]{1,0:T(8,128)S(1)} %copy-done, bf16[240,1024]{1,0:T(8,128)(2,1)S(1)} %collective-permute-done.6.o_ref, bf16[128,3072]{1,0:T(8,128)(2,1)S(1)} %copy-done.1, bf16[128,3072]{1,0:T(8,128)(2,1)S(1)} %collective-permute-done.1.refs_1_, ...), custom_call_target="tpu_custom_call" | custom-call | flops 754974720 | bytes 1887436 | tf_op jit(solution)/shard_map/down/pallas_call | solution.py:167
  129.4 4.1 %all-to-all-start.2 = ((bf16[4,6,240,128]{3,2,1,0:T(8,128)(2,1)}), bf16[4,6,240,128]{3,2,1,0:T(8,128)(2,1)S(1)}, u32[]{:S(2)}, u32[]{:S(2)}) async-start(bf16[4,6,240,128]{3,2,1,0:T(8,128)(2,1)} %down.1), calls=%async_computation.2 | async-start | bytes 2949120 | tf_op jit(solution)/shard_map/all_to_all | solution.py:277
  133.5 0.5 broadcast_xor_fusion._
  134.0 7.1 %shared.1 = bf16[4,2,6,32,128]{4,3,2,1,0:T(8,128)(2,1)} custom-call(s32[4]{0:T(128)} %broadcast_xor_fusion._, bf16[2,2,6,32,128]{4,3,2,1,0:T(8,128)(2,1)} %copy-done.4, bf16[2,2,6,32,128]{4,3,2,1,0:T(8,128)(2,1)} %copy-done.5, bf16[6144,128]{1,0:T(8,128)(2,1)} %g_ref.1, bf16[6144,128]{1,0:T(8,128)(2,1)} %u_ref.1, bf16[128,6144]{1,0:T(8,128)(2,1)} %d_ref.1), custom_call_target="tpu_custom_call" | custom-call | flops 150994944 | bytes 377487 | tf_op jit(solution)/shard_map/shared/pallas_call | solution.py:222
  141.1 0.9 slice.50
  142.1 3.4 %collective-permute-start.11 = (bf16[2,2,6,32,128]{4,3,2,1,0:T(8,128)(2,1)S(1)}, bf16[2,2,6,32,128]{4,3,2,1,0:T(8,128)(2,1)S(1)}, u32[]{:S(2)}, u32[]{:S(2)}) collective-permute-start(bf16[2,2,6,32,128]{4,3,2,1,0:T(8,128)(2,1)S(1)} %slice.50), channel_id=1, source_target_pairs={{0,4},{4,0},{8,12},{12,8},{1,5},{5,1},{9,13},{13,9},{2,6},{6,2},{1... | collective-permute-start | bytes 589832 | tf_op jit(solution)/shard_map/ppermute | solution.py:267
  145.5 5.5 %all-to-all-done.2 = bf16[4,6,240,128]{3,2,1,0:T(8,128)(2,1)S(1)} async-done(((bf16[4,6,240,128]{3,2,1,0:T(8,128)(2,1)}), bf16[4,6,240,128]{3,2,1,0:T(8,128)(2,1)S(1)}, u32[]{:S(2)}, u32[]{:S(2)}) %all-to-all-start.2) | async-done | bytes 1474592 | tf_op jit(solution)/shard_map/all_to_all | solution.py:277
  151.3 0.9 copy.33
  152.1 11.9 %all-to-all-start.3 = ((bf16[48,32,128]{2,1,0:T(8,128)(2,1)}), bf16[48,32,128]{2,1,0:T(8,128)(2,1)S(1)}, u32[]{:S(2)}, u32[]{:S(2)}) async-start(bf16[48,32,128]{2,1,0:T(8,128)(2,1)} %copy.33), calls=%async_computation.3 | async-start | bytes 786432 | tf_op jit(solution)/shard_map/all_to_all | solution.py:277
  164.1 2.2 %collective-permute-start.12 = (bf16[1,2,6,32,128]{4,3,2,1,0:T(8,128)(2,1)S(1)}, bf16[1,2,6,32,128]{4,3,2,1,0:T(8,128)(2,1)S(1)}, u32[]{:S(2)}, u32[]{:S(2)}) collective-permute-start(bf16[1,2,6,32,128]{4,3,2,1,0:T(8,128)(2,1)S(1)} %slice.52), channel_id=1, source_target_pairs={{0,8},{4,12},{8,0},{12,4},{1,9},{5,13},{9,1},{13,5},{2,10},{6,14},... | collective-permute-start | bytes 294920 | tf_op jit(solution)/shard_map/ppermute | solution.py:267
  166.5 4.5 %collective-permute-done.12 = bf16[1,2,6,32,128]{4,3,2,1,0:T(8,128)(2,1)S(1)} collective-permute-done((bf16[1,2,6,32,128]{4,3,2,1,0:T(8,128)(2,1)S(1)}, bf16[1,2,6,32,128]{4,3,2,1,0:T(8,128)(2,1)S(1)}, u32[]{:S(2)}, u32[]{:S(2)}) %collective-permute-start.12) | collective-permute-done | bytes 98336 | tf_op jit(solution)/shard_map/ppermute | solution.py:267
  171.1 2.8 %collective-permute-start.13 = (bf16[6,32,128]{2,1,0:T(8,128)(2,1)S(1)}, bf16[6,32,128]{2,1,0:T(8,128)(2,1)S(1)}, u32[]{:S(2)}, u32[]{:S(2)}) collective-permute-start(bf16[6,32,128]{2,1,0:T(8,128)(2,1)S(1)} %select_bitcast_fusion), channel_id=1, source_target_pairs={{0,2},{2,0},{1,3},{3,1},{4,6},{6,4},{5,7},{7,5},{8,10},{10,8},{9,1... | collective-permute-start | bytes 147464 | tf_op jit(solution)/shard_map/ppermute | solution.py:264
  174.1 0.4 copy.30
  174.6 2.9 %collective-permute-done.13 = bf16[6,32,128]{2,1,0:T(8,128)(2,1)S(1)} collective-permute-done((bf16[6,32,128]{2,1,0:T(8,128)(2,1)S(1)}, bf16[6,32,128]{2,1,0:T(8,128)(2,1)S(1)}, u32[]{:S(2)}, u32[]{:S(2)}) %collective-permute-start.13) | collective-permute-done | bytes 49184 | tf_op jit(solution)/shard_map/ppermute | solution.py:264
  177.5 4.5 %all-to-all-done.3 = bf16[48,32,128]{2,1,0:T(8,128)(2,1)S(1)} async-done(((bf16[48,32,128]{2,1,0:T(8,128)(2,1)}), bf16[48,32,128]{2,1,0:T(8,128)(2,1)S(1)}, u32[]{:S(2)}, u32[]{:S(2)}) %all-to-all-start.3) | async-done | bytes 393248 | tf_op jit(solution)/shard_map/all_to_all | solution.py:277
  181.9 0.7 fusion.8
  182.7 10.2 %collective-permute-start.14 = (f32[3,32,128]{2,1,0:T(8,128)S(1)}, f32[3,32,128]{2,1,0:T(8,128)S(1)}, u32[]{:S(2)}, u32[]{:S(2)}) collective-permute-start(f32[3,32,128]{2,1,0:T(8,128)S(1)} %slice_select_fusion), channel_id=1, source_target_pairs={{0,1},{1,0},{2,3},{3,2},{4,5},{5,4},{6,7},{7,6},{8,9},{9,8},{10,11... | collective-permute-start | bytes 147464 | tf_op jit(solution)/shard_map/ppermute | solution.py:354
  192.8 0.9 collective-permute-done.14
  193.7 0.6 copy_bitcast_fusion.1
  (49 shorter events, 1.6 us)
Async XLA Ops:
  12.4 5.8 %copy-start.6 = (bf16[32,6,128]{2,0,1:T(8,128)(2,1)}, bf16[32,6,128]{2,0,1:T(8,128)(2,1)S(1)}, u32[]{:S(2)}) copy-start(bf16[32,6,128]{2,0,1:T(8,128)(2,1)S(1)} %get-tuple-element.56) | copy-start | bytes 147460
  18.1 34.9 %collective-permute-start = (bf16[6144,128]{1,0:T(8,128)(2,1)}, bf16[6144,128]{1,0:T(8,128)(2,1)S(1)}, u32[]{:S(2)}, u32[]{:S(2)}) collective-permute-start(bf16[6144,128]{1,0:T(8,128)(2,1)} %get-tuple-element.32.refs_0_.refs_4_), channel_id=1, source_target_pairs={{0,1},{1,0},{2,3},{3,2},{4,5},{5,4},{6,7},{7,6},{8,9},{9,8},{10,11... | collective-permute-start | bytes 4718600 | tf_op jit(solution)/shard_map/ppermute | solution.py:270
  20.4 32.6 %all-to-all-start = ((bf16[48,32,128]{2,1,0:T(8,128)(2,1)}), bf16[48,32,128]{2,1,0:T(8,128)(2,1)S(1)}, u32[]{:S(2)}, u32[]{:S(2)}) async-start(bf16[48,32,128]{2,1,0:T(8,128)(2,1)} %bitcast.9), calls=%async_computation | async-start | bytes 786432 | tf_op jit(solution)/shard_map/all_to_all | solution.py:277
  32.2 10.0 %collective-permute-start.1 = (bf16[128,3072]{1,0:T(8,128)(2,1)}, bf16[128,3072]{1,0:T(8,128)(2,1)S(1)}, u32[]{:S(2)}, u32[]{:S(2)}) collective-permute-start(bf16[128,3072]{1,0:T(8,128)(2,1)} %get-tuple-element.33.refs_0_), channel_id=1, source_target_pairs={{0,1},{1,0},{2,3},{3,2},{4,5},{5,4},{6,7},{7,6},{8,9},{9,8},{10,11... | collective-permute-start | bytes 2359304 | tf_op jit(solution)/shard_map/ppermute | solution.py:270
  36.9 27.0 %collective-permute-start.2 = (bf16[3264,128]{1,0:T(8,128)(2,1)}, bf16[3264,128]{1,0:T(8,128)(2,1)}, u32[]{:S(2)}, u32[]{:S(2)}) collective-permute-start(bf16[3264,128]{1,0:T(8,128)(2,1)} %get-tuple-element.36), channel_id=1, source_target_pairs={{0,2},{2,0},{1,3},{3,1},{4,6},{6,4},{5,7},{7,5},{8,10},{10,8},{9,1... | collective-permute-start | bytes 2506760 | tf_op jit(solution)/shard_map/ppermute | solution.py:264
  39.3 41.5 %collective-permute-start.4 = (bf16[3072,128]{1,0:T(8,128)(2,1)}, bf16[3072,128]{1,0:T(8,128)(2,1)}, u32[]{:S(2)}, u32[]{:S(2)}) collective-permute-start(bf16[3072,128]{1,0:T(8,128)(2,1)} %get-tuple-element.37), channel_id=1, source_target_pairs={{0,2},{2,0},{1,3},{3,1},{4,6},{6,4},{5,7},{7,5},{8,10},{10,8},{9,1... | collective-permute-start | bytes 2359304 | tf_op jit(solution)/shard_map/ppermute | solution.py:264
  53.0 1.7 copy-start.2
  54.7 4.5 %copy-start.7 = (bf16[128,3072]{1,0:T(8,128)(2,1)S(1)}, bf16[128,3072]{1,0:T(8,128)(2,1)}, u32[]{:S(2)}) copy-start(bf16[128,3072]{1,0:T(8,128)(2,1)} %get-tuple-element.44) | copy-start | bytes 2359300
  54.7 46.1 %all-to-all-start.1 = ((bf16[4,6,240,128]{3,2,1,0:T(8,128)(2,1)}), bf16[4,6,240,128]{3,2,1,0:T(8,128)(2,1)}, u32[]{:S(2)}, u32[]{:S(2)}) async-start(bf16[4,6,240,128]{3,2,1,0:T(8,128)(2,1)} %broadcast_in_dim.67), calls=%async_computation.1 | async-start | bytes 2949120 | tf_op jit(solution)/shard_map/all_to_all | solution.py:277
  59.2 38.3 %collective-permute-start.7 = (bf16[128,3072]{1,0:T(8,128)(2,1)S(1)}, bf16[128,3072]{1,0:T(8,128)(2,1)S(1)}, u32[]{:S(2)}, u32[]{:S(2)}) collective-permute-start(bf16[128,3072]{1,0:T(8,128)(2,1)S(1)} %copy-done.7), channel_id=1, source_target_pairs={{0,2},{2,0},{1,3},{3,1},{4,6},{6,4},{5,7},{7,5},{8,10},{10,8},{9,1... | collective-permute-start | bytes 2359304 | tf_op jit(solution)/shard_map/ppermute | solution.py:264
  63.9 36.9 %collective-permute-start.3 = (bf16[3264,128]{1,0:T(8,128)(2,1)}, bf16[3264,128]{1,0:T(8,128)(2,1)}, u32[]{:S(2)}, u32[]{:S(2)}) collective-permute-start(bf16[3264,128]{1,0:T(8,128)(2,1)} %collective-permute-done.2.refs_2_), channel_id=1, source_target_pairs={{0,1},{1,0},{2,3},{3,2},{4,5},{5,4},{6,7},{7,6},{8,9},{9,8},{10,11... | collective-permute-start | bytes 2506760 | tf_op jit(solution)/shard_map/ppermute | solution.py:270
  80.8 20.0 %collective-permute-start.5 = (bf16[3072,128]{1,0:T(8,128)(2,1)}, bf16[3072,128]{1,0:T(8,128)(2,1)}, u32[]{:S(2)}, u32[]{:S(2)}) collective-permute-start(bf16[3072,128]{1,0:T(8,128)(2,1)} %collective-permute-done.4.refs_6_), channel_id=1, source_target_pairs={{0,1},{1,0},{2,3},{3,2},{4,5},{5,4},{6,7},{7,6},{8,9},{9,8},{10,11... | collective-permute-start | bytes 2359304 | tf_op jit(solution)/shard_map/ppermute | solution.py:270
  97.5 27.0 %collective-permute-start.8 = (bf16[128,3072]{1,0:T(8,128)(2,1)S(1)}, bf16[128,3072]{1,0:T(8,128)(2,1)S(1)}, u32[]{:S(2)}, u32[]{:S(2)}) collective-permute-start(bf16[128,3072]{1,0:T(8,128)(2,1)S(1)} %collective-permute-done.7.refs_2_), channel_id=1, source_target_pairs={{0,1},{1,0},{2,3},{3,2},{4,5},{5,4},{6,7},{7,6},{8,9},{9,8},{10,11... | collective-permute-start | bytes 2359304 | tf_op jit(solution)/shard_map/ppermute | solution.py:270
  100.8 24.5 %copy-start.1 = (bf16[128,3072]{1,0:T(8,128)(2,1)S(1)}, bf16[128,3072]{1,0:T(8,128)(2,1)}, u32[]{:S(2)}) copy-start(bf16[128,3072]{1,0:T(8,128)(2,1)} %get-tuple-element.33.refs_0_) | copy-start | bytes 2359300
  107.1 17.5 %collective-permute-start.6 = (bf16[240,1024]{1,0:T(8,128)(2,1)}, bf16[240,1024]{1,0:T(8,128)(2,1)S(1)}, u32[]{:S(2)}, u32[]{:S(2)}) collective-permute-start(bf16[240,1024]{1,0:T(8,128)(2,1)} %get-tuple-element.43), channel_id=1, source_target_pairs={{0,2},{2,0},{1,3},{3,1},{4,6},{6,4},{5,7},{7,5},{8,10},{10,8},{9,1... | collective-permute-start | bytes 1474568 | tf_op jit(solution)/shard_map/ppermute | solution.py:264
  109.9 7.5 %collective-permute-start.9 = (bf16[1,2,6,32,128]{4,3,2,1,0:T(8,128)(2,1)S(1)}, bf16[1,2,6,32,128]{4,3,2,1,0:T(8,128)(2,1)S(1)}, u32[]{:S(2)}, u32[]{:S(2)}) collective-permute-start(bf16[1,2,6,32,128]{4,3,2,1,0:T(8,128)(2,1)S(1)} %maximum_select_fusion), channel_id=1, source_target_pairs={{0,8},{4,12},{8,0},{12,4},{1,9},{5,13},{9,1},{13,5},{2,10},{6,14},... | collective-permute-start | bytes 294920 | tf_op jit(solution)/shard_map/ppermute | solution.py:267
  117.3 12.0 %copy-start.4 = (bf16[2,2,6,32,128]{4,3,2,1,0:T(8,128)(2,1)}, bf16[2,2,6,32,128]{4,3,2,1,0:T(8,128)(2,1)S(1)}, u32[]{:S(2)}) copy-start(bf16[2,2,6,32,128]{4,3,2,1,0:T(8,128)(2,1)S(1)} %pad_maximum_fusion.x_ref) | copy-start | bytes 589828
  117.3 7.2 %collective-permute-start.10 = (bf16[2,2,6,32,128]{4,3,2,1,0:T(8,128)(2,1)S(1)}, bf16[2,2,6,32,128]{4,3,2,1,0:T(8,128)(2,1)S(1)}, u32[]{:S(2)}, u32[]{:S(2)}) collective-permute-start(bf16[2,2,6,32,128]{4,3,2,1,0:T(8,128)(2,1)S(1)} %pad_maximum_fusion.x_ref), channel_id=1, source_target_pairs={{0,4},{4,0},{8,12},{12,8},{1,5},{5,1},{9,13},{13,9},{2,6},{6,2},{1... | collective-permute-start | bytes 589832 | tf_op jit(solution)/shard_map/ppermute | solution.py:267
  124.5 0.7 copy-start.5
  125.2 1.2 copy-start
  129.4 4.1 %copy-start.8 = (s32[4]{0:T(128)S(1)}, s32[4]{0:T(128)}, u32[]{:S(2)}) copy-start(s32[4]{0:T(128)} %constant.63.clone) | copy-start | bytes 52
  129.4 21.6 %all-to-all-start.2 = ((bf16[4,6,240,128]{3,2,1,0:T(8,128)(2,1)}), bf16[4,6,240,128]{3,2,1,0:T(8,128)(2,1)S(1)}, u32[]{:S(2)}, u32[]{:S(2)}) async-start(bf16[4,6,240,128]{3,2,1,0:T(8,128)(2,1)} %down.1), calls=%async_computation.2 | async-start | bytes 2949120 | tf_op jit(solution)/shard_map/all_to_all | solution.py:277
  142.1 22.0 %collective-permute-start.11 = (bf16[2,2,6,32,128]{4,3,2,1,0:T(8,128)(2,1)S(1)}, bf16[2,2,6,32,128]{4,3,2,1,0:T(8,128)(2,1)S(1)}, u32[]{:S(2)}, u32[]{:S(2)}) collective-permute-start(bf16[2,2,6,32,128]{4,3,2,1,0:T(8,128)(2,1)S(1)} %slice.50), channel_id=1, source_target_pairs={{0,4},{4,0},{8,12},{12,8},{1,5},{5,1},{9,13},{13,9},{2,6},{6,2},{1... | collective-permute-start | bytes 589832 | tf_op jit(solution)/shard_map/ppermute | solution.py:267
  151.2 12.8 %copy-start.3 = (bf16[4,2,6,32,128]{4,3,2,1,0:T(8,128)(2,1)S(1)}, bf16[4,2,6,32,128]{4,3,2,1,0:T(8,128)(2,1)}, u32[]{:S(2)}) copy-start(bf16[4,2,6,32,128]{4,3,2,1,0:T(8,128)(2,1)} %shared.1) | copy-start | bytes 1179652
  152.1 29.8 %all-to-all-start.3 = ((bf16[48,32,128]{2,1,0:T(8,128)(2,1)}), bf16[48,32,128]{2,1,0:T(8,128)(2,1)S(1)}, u32[]{:S(2)}, u32[]{:S(2)}) async-start(bf16[48,32,128]{2,1,0:T(8,128)(2,1)} %copy.33), calls=%async_computation.3 | async-start | bytes 786432 | tf_op jit(solution)/shard_map/all_to_all | solution.py:277
  164.1 6.9 %collective-permute-start.12 = (bf16[1,2,6,32,128]{4,3,2,1,0:T(8,128)(2,1)S(1)}, bf16[1,2,6,32,128]{4,3,2,1,0:T(8,128)(2,1)S(1)}, u32[]{:S(2)}, u32[]{:S(2)}) collective-permute-start(bf16[1,2,6,32,128]{4,3,2,1,0:T(8,128)(2,1)S(1)} %slice.52), channel_id=1, source_target_pairs={{0,8},{4,12},{8,0},{12,4},{1,9},{5,13},{9,1},{13,5},{2,10},{6,14},... | collective-permute-start | bytes 294920 | tf_op jit(solution)/shard_map/ppermute | solution.py:267
  171.1 6.4 %collective-permute-start.13 = (bf16[6,32,128]{2,1,0:T(8,128)(2,1)S(1)}, bf16[6,32,128]{2,1,0:T(8,128)(2,1)S(1)}, u32[]{:S(2)}, u32[]{:S(2)}) collective-permute-start(bf16[6,32,128]{2,1,0:T(8,128)(2,1)S(1)} %select_bitcast_fusion), channel_id=1, source_target_pairs={{0,2},{2,0},{1,3},{3,1},{4,6},{6,4},{5,7},{7,5},{8,10},{10,8},{9,1... | collective-permute-start | bytes 147464 | tf_op jit(solution)/shard_map/ppermute | solution.py:264
  182.7 11.0 %collective-permute-start.14 = (f32[3,32,128]{2,1,0:T(8,128)S(1)}, f32[3,32,128]{2,1,0:T(8,128)S(1)}, u32[]{:S(2)}, u32[]{:S(2)}) collective-permute-start(f32[3,32,128]{2,1,0:T(8,128)S(1)} %slice_select_fusion), channel_id=1, source_target_pairs={{0,1},{1,0},{2,3},{3,2},{4,5},{5,4},{6,7},{7,6},{8,9},{9,8},{10,11... | collective-permute-start | bytes 147464 | tf_op jit(solution)/shard_map/ppermute | solution.py:354

commit v4 on v3

--- a/solution.py
+++ b/solution.py
@@ -111,13 +111,17 @@
         w, acc, sent = refs[: len(ins)], refs[-2], refs[-1]
         i = pl.program_id(0)
 
-        @pl.when(i == 0)
-        def _():
-            acc[...] = jnp.zeros_like(acc)
-
         lines = jnp.concatenate([x_ref[0, j] for j in range(chunks)], axis=1)
         weights = jnp.concatenate([r[...] for r in w], axis=1)
-        acc[...] += jnp.dot(lines, weights, preferred_element_type=jnp.float32)
+        step = jnp.dot(lines, weights, preferred_element_type=jnp.float32)
+
+        @pl.when(i == 0)
+        def _():
+            acc[...] = step
+
+        @pl.when(i > 0)
+        def _():
+            acc[...] += step
 
         @pl.when(i == chips - 1)
         def _():
@@ -137,7 +141,7 @@
             jax.ShapeDtypeStruct((rows, wide), jnp.bfloat16),
         ],
         cost_estimate=estimate(2 * rows * chips * width * wide),
-        compiler_params=PARAMS,
+        compiler_params=SMALL,
         name="partial",
     )(x, *ins)
 
@@ -313,6 +317,7 @@
     theirs = got[xs * width :].reshape(stacked.shape)
     whole = jnp.where(yi == 0, jnp.stack([stacked, theirs]), jnp.stack([theirs, stacked]))[None]
     whole_x = to_x(whole, 2)
+    got_up, partner_got = lax.optimization_barrier((got_up, partner_got))
     partner_got_up = to_c(got_up)
     gathered, partner_got, partner_got_up = lax.optimization_barrier((gathered, partner_got, partner_got_up))
     sums, sent = partial_sums(

time: 196 us -> 190 us (0.969)
  waiting for transfers between devices: 65.8 us -> 63.6 us
  starting transfers between devices: 82.2 us -> 80.1 us
    all_to_all x4, waiting for transfers between devices: 20.7 us -> 11.5 us  [exchange(): return lax.all_to_all(v, axes, split_axis=0, concat_axis=0, tiled=True)]
    ppermute x4, starting transfers between devices: 13.4 us -> 9.4 us  [to_x(): return lax.ppermute(v, 'x', [(i, i ^ bit) for i in range(xs)])]
    ppermute x4, waiting for transfers between devices: 11.4 us -> 15.3 us  [to_x(): return lax.ppermute(v, 'x', [(i, i ^ bit) for i in range(xs)])]
    ppermute x5, waiting for transfers between devices: 32.8 us -> 35.8 us  [to_y(): return lax.ppermute(v, 'y', swap)]
where the time goes in v4:
time: 190 us; the launch traced here: 189 us
  starting transfers between devices  80.1 us (42%)
  waiting for transfers between devices  63.6 us (33%)
  Pallas kernels  21.9 us (12%)
  blocking collectives  12.2 us (6%)
  local copies, waits for them, and re-layouts  5.67 us (3%)
  other arithmetic  2.93 us (2%)
  matrix products  2.01 us (1%)
    ppermute x5, waiting for transfers between devices, to_y(): return lax.ppermute(v, 'y', swap)  35.8 us
    all_to_all x4, starting transfers between devices, exchange(): return lax.all_to_all(v, axes, split_axis=0, concat_axis=0, tiled=True)  34.1 us
    ppermute x4, waiting for transfers between devices, to_x(): return lax.ppermute(v, 'x', [(i, i ^ bit) for i in range(xs)])  15.3 us
    ppermute x5, starting transfers between devices, to_c(): return lax.ppermute(v, 'c', swap)  14.4 us
    all_gather x1, blocking collectives, local(): pair = lax.all_gather(tokens, 'c', axis=1, tiled=True)  12.2 us
    ppermute x5, starting transfers between devices, to_y(): return lax.ppermute(v, 'y', swap)  12.2 us
    all_to_all x4, waiting for transfers between devices, exchange(): return lax.all_to_all(v, axes, split_axis=0, concat_axis=0, tiled=True)  11.5 us
    ppermute x1, starting transfers between devices, local(): result = keep + lax.ppermute(send, 'c', swap)  10 us
  transfers between devices with their start and end apart: 19, of which 11 were waited for; matrix products, arithmetic and copies ran while one was open for 3% of the time, Pallas kernels for 8%

profile of v4, /device:TPU:1, one launch (start us, length us, event | category | flops | bytes accessed | tf_op | source)
XLA Modules:
  0.0 188.9 jit_solution(15448251037270377709)
XLA Ops:
  0.2 12.2 %all_gather.3 = bf16[32,768]{1,0:T(8,128)(2,1)S(1)} all-gather(bf16[32,384]{1,0:T(8,128)(2,1)} %param.10), channel_id=1, replica_groups=mesh['ep'=48,'x'=4,'y'=2,'c'=2] {'c'}, dimensions={1}, use_global_device_ids=true | all-gather | bytes 73728 | tf_op jit(solution)/shard_map/all_gather | solution.py:290
  12.4 0.9 convert_reduce_fusion
  13.7 1.2 convolution_convert_fusion
  14.9 3.2 %shard_map.100 = (bf16[6144,128]{1,0:T(8,128)(2,1)}, bf16[128,3072]{1,0:T(8,128)(2,1)}, bf16[128,3072]{1,0:T(8,128)(2,1)}) custom-call(s32[1]{0:T(128)} %bitcast.10.y_ref, bf16[6144,128]{1,0:T(8,128)(2,1)} %bitcast.56, bf16[6144,128]{1,0:T(8,128)(2,1)} %bitcast.58, bf16[128,6144]{1,0:T(8,128)(2,1)} %bitcast.55), custom_call_target="tpu_custom_call" | custom-call | flops 1000000000 | bytes 2500000 | tf_op jit(solution)/shard_map/pallas_call | solution.py:38
  18.2 2.4 %collective-permute-start = (bf16[6144,128]{1,0:T(8,128)(2,1)}, bf16[6144,128]{1,0:T(8,128)(2,1)S(1)}, u32[]{:S(2)}, u32[]{:S(2)}) collective-permute-start(bf16[6144,128]{1,0:T(8,128)(2,1)} %get-tuple-element.34.refs_0_.refs_4_), channel_id=1, source_target_pairs={{0,1},{1,0},{2,3},{3,2},{4,5},{5,4},{6,7},{7,6},{8,9},{9,8},{10,11... | collective-permute-start | bytes 4718600 | tf_op jit(solution)/shard_map/ppermute | solution.py:274
  20.6 2.4 %shard_map.101 = (bf16[3264,128]{1,0:T(8,128)(2,1)}, bf16[3072,128]{1,0:T(8,128)(2,1)}) custom-call(s32[1]{0:T(128)} %bitcast.10.y_ref, bf16[6144,128]{1,0:T(8,128)(2,1)} %bitcast.57, bf16[6144,128]{1,0:T(8,128)(2,1)} %bitcast.59, bf16[192,128]{1,0:T(8,128)(2,1)} %bitcast.67), custom_call_target="tpu_custom_call" | custom-call | flops 1000000000 | bytes 2500000 | tf_op jit(solution)/shard_map/pallas_call | solution.py:38
  22.9 1.9 %collective-permute-start.3 = (bf16[3264,128]{1,0:T(8,128)(2,1)}, bf16[3264,128]{1,0:T(8,128)(2,1)}, u32[]{:S(2)}, u32[]{:S(2)}) collective-permute-start(bf16[3264,128]{1,0:T(8,128)(2,1)} %get-tuple-element.39), channel_id=1, source_target_pairs={{0,2},{2,0},{1,3},{3,1},{4,6},{6,4},{5,7},{7,5},{8,10},{10,8},{9,1... | collective-permute-start | bytes 2506760 | tf_op jit(solution)/shard_map/ppermute | solution.py:268
  24.8 12.2 %all-to-all-start = ((bf16[48,32,128]{2,1,0:T(8,128)(2,1)}), bf16[48,32,128]{2,1,0:T(8,128)(2,1)S(1)}, u32[]{:S(2)}, u32[]{:S(2)}) async-start(bf16[48,32,128]{2,1,0:T(8,128)(2,1)} %bitcast.9), calls=%async_computation | async-start | bytes 786432 | tf_op jit(solution)/shard_map/all_to_all | solution.py:281
  37.1 2.6 %collective-permute-start.1 = (bf16[128,3072]{1,0:T(8,128)(2,1)S(1)}, bf16[128,3072]{1,0:T(8,128)(2,1)S(1)}, u32[]{:S(2)}, u32[]{:S(2)}) collective-permute-start(bf16[128,3072]{1,0:T(8,128)(2,1)S(1)} %copy-done.1), channel_id=1, source_target_pairs={{0,1},{1,0},{2,3},{3,2},{4,5},{5,4},{6,7},{7,6},{8,9},{9,8},{10,11... | collective-permute-start | bytes 2359304 | tf_op jit(solution)/shard_map/ppermute | solution.py:274
  39.7 11.2 %collective-permute-done.3.refs_2_ = bf16[3264,128]{1,0:T(8,128)(2,1)} collective-permute-done((bf16[3264,128]{1,0:T(8,128)(2,1)}, bf16[3264,128]{1,0:T(8,128)(2,1)}, u32[]{:S(2)}, u32[]{:S(2)}) %collective-permute-start.3) | collective-permute-done | bytes 835616 | tf_op jit(solution)/shard_map/ppermute | solution.py:268
  51.0 3.4 %collective-permute-start.4 = (bf16[3264,128]{1,0:T(8,128)(2,1)}, bf16[3264,128]{1,0:T(8,128)(2,1)}, u32[]{:S(2)}, u32[]{:S(2)}) collective-permute-start(bf16[3264,128]{1,0:T(8,128)(2,1)} %collective-permute-done.3.refs_2_), channel_id=1, source_target_pairs={{0,1},{1,0},{2,3},{3,2},{4,5},{5,4},{6,7},{7,6},{8,9},{9,8},{10,11... | collective-permute-start | bytes 2506760 | tf_op jit(solution)/shard_map/ppermute | solution.py:274
  54.4 1.9 %collective-permute-start.2 = (bf16[3072,128]{1,0:T(8,128)(2,1)}, bf16[3072,128]{1,0:T(8,128)(2,1)}, u32[]{:S(2)}, u32[]{:S(2)}) collective-permute-start(bf16[3072,128]{1,0:T(8,128)(2,1)} %get-tuple-element.38), channel_id=1, source_target_pairs={{0,2},{2,0},{1,3},{3,1},{4,6},{6,4},{5,7},{7,5},{8,10},{10,8},{9,1... | collective-permute-start | bytes 2359304 | tf_op jit(solution)/shard_map/ppermute | solution.py:268
  56.3 0.9 copy-done.3
  57.2 0.9 all-to-all-done
  58.3 1.3 broadcast_in_dim.67
  59.6 4.5 %all-to-all-start.1 = ((bf16[4,6,240,128]{3,2,1,0:T(8,128)(2,1)}), bf16[4,6,240,128]{3,2,1,0:T(8,128)(2,1)}, u32[]{:S(2)}, u32[]{:S(2)}) async-start(bf16[4,6,240,128]{3,2,1,0:T(8,128)(2,1)} %broadcast_in_dim.67), calls=%async_computation.1 | async-start | bytes 2949120 | tf_op jit(solution)/shard_map/all_to_all | solution.py:281
  64.1 3.0 %collective-permute-start.7 = (bf16[128,3072]{1,0:T(8,128)(2,1)}, bf16[128,3072]{1,0:T(8,128)(2,1)}, u32[]{:S(2)}, u32[]{:S(2)}) collective-permute-start(bf16[128,3072]{1,0:T(8,128)(2,1)} %get-tuple-element.48), channel_id=1, source_target_pairs={{0,2},{2,0},{1,3},{3,1},{4,6},{6,4},{5,7},{7,5},{8,10},{10,8},{9,1... | collective-permute-start | bytes 2359304 | tf_op jit(solution)/shard_map/ppermute | solution.py:268
  67.1 8.6 %collective-permute-done.2.refs_6_ = bf16[3072,128]{1,0:T(8,128)(2,1)} collective-permute-done((bf16[3072,128]{1,0:T(8,128)(2,1)}, bf16[3072,128]{1,0:T(8,128)(2,1)}, u32[]{:S(2)}, u32[]{:S(2)}) %collective-permute-start.2) | collective-permute-done | bytes 786464 | tf_op jit(solution)/shard_map/ppermute | solution.py:268
  75.7 3.2 %collective-permute-start.5 = (bf16[3072,128]{1,0:T(8,128)(2,1)}, bf16[3072,128]{1,0:T(8,128)(2,1)}, u32[]{:S(2)}, u32[]{:S(2)}) collective-permute-start(bf16[3072,128]{1,0:T(8,128)(2,1)} %collective-permute-done.2.refs_6_), channel_id=1, source_target_pairs={{0,1},{1,0},{2,3},{3,2},{4,5},{5,4},{6,7},{7,6},{8,9},{9,8},{10,11... | collective-permute-start | bytes 2359304 | tf_op jit(solution)/shard_map/ppermute | solution.py:274
  78.9 13.6 %collective-permute-done.7.refs_2_ = bf16[128,3072]{1,0:T(8,128)(2,1)} collective-permute-done((bf16[128,3072]{1,0:T(8,128)(2,1)}, bf16[128,3072]{1,0:T(8,128)(2,1)}, u32[]{:S(2)}, u32[]{:S(2)}) %collective-permute-start.7) | collective-permute-done | bytes 786464 | tf_op jit(solution)/shard_map/ppermute | solution.py:268
  92.5 2.8 %collective-permute-start.8 = (bf16[128,3072]{1,0:T(8,128)(2,1)}, bf16[128,3072]{1,0:T(8,128)(2,1)}, u32[]{:S(2)}, u32[]{:S(2)}) collective-permute-start(bf16[128,3072]{1,0:T(8,128)(2,1)} %collective-permute-done.7.refs_2_), channel_id=1, source_target_pairs={{0,1},{1,0},{2,3},{3,2},{4,5},{5,4},{6,7},{7,6},{8,9},{9,8},{10,11... | collective-permute-start | bytes 2359304 | tf_op jit(solution)/shard_map/ppermute | solution.py:274
  95.3 0.8 slice.49
  96.1 4.7 %partial.1 = (f32[240,1024]{1,0:T(8,128)S(1)}, bf16[240,1024]{1,0:T(8,128)(2,1)S(1)}) custom-call(bf16[4,6,240,128]{3,2,1,0:T(8,128)(2,1)} %all-to-all-done.1.x_ref, bf16[6144,128]{1,0:T(8,128)(2,1)S(1)} %copy-done, bf16[6144,128]{1,0:T(8,128)(2,1)S(1)} %collective-permute-done.refs_1_.refs_5_, bf16[3264,128]{1,0:T(8,128)(2,1)} %collective-permute-done.3.refs_2_, ...), custom_call_target="tpu_custom_call" | custom-call | flops 1509949440 | bytes 3774873 | tf_op jit(solution)/shard_map/partial/pallas_call | solution.py:131
  100.8 2.3 %collective-permute-start.6 = (bf16[240,1024]{1,0:T(8,128)(2,1)S(1)}, bf16[240,1024]{1,0:T(8,128)(2,1)S(1)}, u32[]{:S(2)}, u32[]{:S(2)}) collective-permute-start(bf16[240,1024]{1,0:T(8,128)(2,1)S(1)} %get-tuple-element.47), channel_id=1, source_target_pairs={{0,2},{2,0},{1,3},{3,1},{4,6},{6,4},{5,7},{7,5},{8,10},{10,8},{9,1... | collective-permute-start | bytes 1474568 | tf_op jit(solution)/shard_map/ppermute | solution.py:268
  103.2 1.9 %collective-permute-start.9 = (bf16[1,2,6,32,128]{4,3,2,1,0:T(8,128)(2,1)S(1)}, bf16[1,2,6,32,128]{4,3,2,1,0:T(8,128)(2,1)S(1)}, u32[]{:S(2)}, u32[]{:S(2)}) collective-permute-start(bf16[1,2,6,32,128]{4,3,2,1,0:T(8,128)(2,1)S(1)} %maximum_select_fusion), channel_id=1, source_target_pairs={{0,8},{4,12},{8,0},{12,4},{1,9},{5,13},{9,1},{13,5},{2,10},{6,14},... | collective-permute-start | bytes 294920 | tf_op jit(solution)/shard_map/ppermute | solution.py:271
  105.1 5.5 %collective-permute-done.9 = bf16[1,2,6,32,128]{4,3,2,1,0:T(8,128)(2,1)S(1)} collective-permute-done((bf16[1,2,6,32,128]{4,3,2,1,0:T(8,128)(2,1)S(1)}, bf16[1,2,6,32,128]{4,3,2,1,0:T(8,128)(2,1)S(1)}, u32[]{:S(2)}, u32[]{:S(2)}) %collective-permute-start.9) | collective-permute-done | bytes 98336 | tf_op jit(solution)/shard_map/ppermute | solution.py:271
  110.7 1.9 %collective-permute-start.10 = (bf16[2,2,6,32,128]{4,3,2,1,0:T(8,128)(2,1)S(1)}, bf16[2,2,6,32,128]{4,3,2,1,0:T(8,128)(2,1)S(1)}, u32[]{:S(2)}, u32[]{:S(2)}) collective-permute-start(bf16[2,2,6,32,128]{4,3,2,1,0:T(8,128)(2,1)S(1)} %pad_maximum_fusion.x_ref), channel_id=1, source_target_pairs={{0,4},{4,0},{8,12},{12,8},{1,5},{5,1},{9,13},{13,9},{2,6},{6,2},{1... | collective-permute-start | bytes 589832 | tf_op jit(solution)/shard_map/ppermute | solution.py:271
  112.6 5.3 %collective-permute-done.10.r_ref = bf16[2,2,6,32,128]{4,3,2,1,0:T(8,128)(2,1)S(1)} collective-permute-done((bf16[2,2,6,32,128]{4,3,2,1,0:T(8,128)(2,1)S(1)}, bf16[2,2,6,32,128]{4,3,2,1,0:T(8,128)(2,1)S(1)}, u32[]{:S(2)}, u32[]{:S(2)}) %collective-permute-start.10) | collective-permute-done | bytes 196640 | tf_op jit(solution)/shard_map/ppermute | solution.py:271
  117.9 4.5 %down.1 = bf16[4,6,240,128]{3,2,1,0:T(8,128)(2,1)} custom-call(f32[240,1024]{1,0:T(8,128)S(1)} %get-tuple-element.46.s_ref, bf16[240,1024]{1,0:T(8,128)(2,1)S(1)} %collective-permute-done.6.o_ref, bf16[128,3072]{1,0:T(8,128)(2,1)S(1)} %copy-done.2, bf16[128,3072]{1,0:T(8,128)(2,1)S(1)} %copy-done.4, bf16[128,3072]{1,0:T(8,128)(2,1)} %collective-permute-done.7.refs_2_, ...), custom_call_target="tpu_custom_call" | custom-call | flops 754974720 | bytes 1887436 | tf_op jit(solution)/shard_map/down/pallas_call | solution.py:171
  122.5 3.6 %all-to-all-start.2 = ((bf16[4,6,240,128]{3,2,1,0:T(8,128)(2,1)}), bf16[4,6,240,128]{3,2,1,0:T(8,128)(2,1)S(1)}, u32[]{:S(2)}, u32[]{:S(2)}) async-start(bf16[4,6,240,128]{3,2,1,0:T(8,128)(2,1)} %down.1), calls=%async_computation.2 | async-start | bytes 2949120 | tf_op jit(solution)/shard_map/all_to_all | solution.py:281
  126.0 0.5 broadcast_xor_fusion._
  126.6 7.1 %shared.1 = bf16[4,2,6,32,128]{4,3,2,1,0:T(8,128)(2,1)} custom-call(s32[4]{0:T(128)} %broadcast_xor_fusion._, bf16[2,2,6,32,128]{4,3,2,1,0:T(8,128)(2,1)} %copy-done.6, bf16[2,2,6,32,128]{4,3,2,1,0:T(8,128)(2,1)} %copy-done.7, bf16[6144,128]{1,0:T(8,128)(2,1)} %g_ref.1, bf16[6144,128]{1,0:T(8,128)(2,1)} %u_ref.1, bf16[128,6144]{1,0:T(8,128)(2,1)} %d_ref.1), custom_call_target="tpu_custom_call" | custom-call | flops 150994944 | bytes 377487 | tf_op jit(solution)/shard_map/shared/pallas_call | solution.py:226
  133.7 0.9 slice.50
  134.6 3.3 %collective-permute-start.11 = (bf16[2,2,6,32,128]{4,3,2,1,0:T(8,128)(2,1)S(1)}, bf16[2,2,6,32,128]{4,3,2,1,0:T(8,128)(2,1)S(1)}, u32[]{:S(2)}, u32[]{:S(2)}) collective-permute-start(bf16[2,2,6,32,128]{4,3,2,1,0:T(8,128)(2,1)S(1)} %slice.50), channel_id=1, source_target_pairs={{0,4},{4,0},{8,12},{12,8},{1,5},{5,1},{9,13},{13,9},{2,6},{6,2},{1... | collective-permute-start | bytes 589832 | tf_op jit(solution)/shard_map/ppermute | solution.py:271
  138.0 5.8 %all-to-all-done.2 = bf16[4,6,240,128]{3,2,1,0:T(8,128)(2,1)S(1)} async-done(((bf16[4,6,240,128]{3,2,1,0:T(8,128)(2,1)}), bf16[4,6,240,128]{3,2,1,0:T(8,128)(2,1)S(1)}, u32[]{:S(2)}, u32[]{:S(2)}) %all-to-all-start.2) | async-done | bytes 1474592 | tf_op jit(solution)/shard_map/all_to_all | solution.py:281
  143.7 0.3 reduce_sum.32
  144.1 0.9 copy.33
  144.9 13.8 %all-to-all-start.3 = ((bf16[48,32,128]{2,1,0:T(8,128)(2,1)}), bf16[48,32,128]{2,1,0:T(8,128)(2,1)S(1)}, u32[]{:S(2)}, u32[]{:S(2)}) async-start(bf16[48,32,128]{2,1,0:T(8,128)(2,1)} %copy.33), calls=%async_computation.3 | async-start | bytes 786432 | tf_op jit(solution)/shard_map/all_to_all | solution.py:281
  158.8 2.2 %collective-permute-start.12 = (bf16[1,2,6,32,128]{4,3,2,1,0:T(8,128)(2,1)S(1)}, bf16[1,2,6,32,128]{4,3,2,1,0:T(8,128)(2,1)S(1)}, u32[]{:S(2)}, u32[]{:S(2)}) collective-permute-start(bf16[1,2,6,32,128]{4,3,2,1,0:T(8,128)(2,1)S(1)} %slice.52), channel_id=1, source_target_pairs={{0,8},{4,12},{8,0},{12,4},{1,9},{5,13},{9,1},{13,5},{2,10},{6,14},... | collective-permute-start | bytes 294920 | tf_op jit(solution)/shard_map/ppermute | solution.py:271
  161.2 4.5 %collective-permute-done.12 = bf16[1,2,6,32,128]{4,3,2,1,0:T(8,128)(2,1)S(1)} collective-permute-done((bf16[1,2,6,32,128]{4,3,2,1,0:T(8,128)(2,1)S(1)}, bf16[1,2,6,32,128]{4,3,2,1,0:T(8,128)(2,1)S(1)}, u32[]{:S(2)}, u32[]{:S(2)}) %collective-permute-start.12) | collective-permute-done | bytes 98336 | tf_op jit(solution)/shard_map/ppermute | solution.py:271
  165.8 3.0 %collective-permute-start.13 = (bf16[6,32,128]{2,1,0:T(8,128)(2,1)S(1)}, bf16[6,32,128]{2,1,0:T(8,128)(2,1)S(1)}, u32[]{:S(2)}, u32[]{:S(2)}) collective-permute-start(bf16[6,32,128]{2,1,0:T(8,128)(2,1)S(1)} %select_bitcast_fusion), channel_id=1, source_target_pairs={{0,2},{2,0},{1,3},{3,1},{4,6},{6,4},{5,7},{7,5},{8,10},{10,8},{9,1... | collective-permute-start | bytes 147464 | tf_op jit(solution)/shard_map/ppermute | solution.py:268
  169.0 0.4 copy.30
  169.4 2.4 %collective-permute-done.13 = bf16[6,32,128]{2,1,0:T(8,128)(2,1)S(1)} collective-permute-done((bf16[6,32,128]{2,1,0:T(8,128)(2,1)S(1)}, bf16[6,32,128]{2,1,0:T(8,128)(2,1)S(1)}, u32[]{:S(2)}, u32[]{:S(2)}) %collective-permute-start.13) | collective-permute-done | bytes 49184 | tf_op jit(solution)/shard_map/ppermute | solution.py:268
  171.9 4.8 %all-to-all-done.3 = bf16[48,32,128]{2,1,0:T(8,128)(2,1)S(1)} async-done(((bf16[48,32,128]{2,1,0:T(8,128)(2,1)}), bf16[48,32,128]{2,1,0:T(8,128)(2,1)S(1)}, u32[]{:S(2)}, u32[]{:S(2)}) %all-to-all-start.3) | async-done | bytes 393248 | tf_op jit(solution)/shard_map/all_to_all | solution.py:281
  176.7 0.7 fusion.8
  177.4 10.0 %collective-permute-start.14 = (f32[3,32,128]{2,1,0:T(8,128)S(1)}, f32[3,32,128]{2,1,0:T(8,128)S(1)}, u32[]{:S(2)}, u32[]{:S(2)}) collective-permute-start(f32[3,32,128]{2,1,0:T(8,128)S(1)} %slice_select_fusion), channel_id=1, source_target_pairs={{0,1},{1,0},{2,3},{3,2},{4,5},{5,4},{6,7},{7,6},{8,9},{9,8},{10,11... | collective-permute-start | bytes 147464 | tf_op jit(solution)/shard_map/ppermute | solution.py:359
  187.4 0.9 collective-permute-done.14
  188.3 0.6 copy_bitcast_fusion.1
  (51 shorter events, 1.3 us)
Async XLA Ops:
  12.4 5.8 %copy-start.8 = (bf16[32,6,128]{2,0,1:T(8,128)(2,1)}, bf16[32,6,128]{2,0,1:T(8,128)(2,1)S(1)}, u32[]{:S(2)}) copy-start(bf16[32,6,128]{2,0,1:T(8,128)(2,1)S(1)} %get-tuple-element.60) | copy-start | bytes 147460
  18.1 18.9 %copy-start.1 = (bf16[128,3072]{1,0:T(8,128)(2,1)S(1)}, bf16[128,3072]{1,0:T(8,128)(2,1)}, u32[]{:S(2)}) copy-start(bf16[128,3072]{1,0:T(8,128)(2,1)} %get-tuple-element.35.refs_0_) | copy-start | bytes 2359300
  18.2 40.0 %collective-permute-start = (bf16[6144,128]{1,0:T(8,128)(2,1)}, bf16[6144,128]{1,0:T(8,128)(2,1)S(1)}, u32[]{:S(2)}, u32[]{:S(2)}) collective-permute-start(bf16[6144,128]{1,0:T(8,128)(2,1)} %get-tuple-element.34.refs_0_.refs_4_), channel_id=1, source_target_pairs={{0,1},{1,0},{2,3},{3,2},{4,5},{5,4},{6,7},{7,6},{8,9},{9,8},{10,11... | collective-permute-start | bytes 4718600 | tf_op jit(solution)/shard_map/ppermute | solution.py:274
  22.9 28.0 %collective-permute-start.3 = (bf16[3264,128]{1,0:T(8,128)(2,1)}, bf16[3264,128]{1,0:T(8,128)(2,1)}, u32[]{:S(2)}, u32[]{:S(2)}) collective-permute-start(bf16[3264,128]{1,0:T(8,128)(2,1)} %get-tuple-element.39), channel_id=1, source_target_pairs={{0,2},{2,0},{1,3},{3,1},{4,6},{6,4},{5,7},{7,5},{8,10},{10,8},{9,1... | collective-permute-start | bytes 2506760 | tf_op jit(solution)/shard_map/ppermute | solution.py:268
  24.8 33.3 %all-to-all-start = ((bf16[48,32,128]{2,1,0:T(8,128)(2,1)}), bf16[48,32,128]{2,1,0:T(8,128)(2,1)S(1)}, u32[]{:S(2)}, u32[]{:S(2)}) async-start(bf16[48,32,128]{2,1,0:T(8,128)(2,1)} %bitcast.9), calls=%async_computation | async-start | bytes 786432 | tf_op jit(solution)/shard_map/all_to_all | solution.py:281
  37.1 19.2 %collective-permute-start.1 = (bf16[128,3072]{1,0:T(8,128)(2,1)S(1)}, bf16[128,3072]{1,0:T(8,128)(2,1)S(1)}, u32[]{:S(2)}, u32[]{:S(2)}) collective-permute-start(bf16[128,3072]{1,0:T(8,128)(2,1)S(1)} %copy-done.1), channel_id=1, source_target_pairs={{0,1},{1,0},{2,3},{3,2},{4,5},{5,4},{6,7},{7,6},{8,9},{9,8},{10,11... | collective-permute-start | bytes 2359304 | tf_op jit(solution)/shard_map/ppermute | solution.py:274
  51.0 24.7 %collective-permute-start.4 = (bf16[3264,128]{1,0:T(8,128)(2,1)}, bf16[3264,128]{1,0:T(8,128)(2,1)}, u32[]{:S(2)}, u32[]{:S(2)}) collective-permute-start(bf16[3264,128]{1,0:T(8,128)(2,1)} %collective-permute-done.3.refs_2_), channel_id=1, source_target_pairs={{0,1},{1,0},{2,3},{3,2},{4,5},{5,4},{6,7},{7,6},{8,9},{9,8},{10,11... | collective-permute-start | bytes 2506760 | tf_op jit(solution)/shard_map/ppermute | solution.py:274
  54.4 21.3 %collective-permute-start.2 = (bf16[3072,128]{1,0:T(8,128)(2,1)}, bf16[3072,128]{1,0:T(8,128)(2,1)}, u32[]{:S(2)}, u32[]{:S(2)}) collective-permute-start(bf16[3072,128]{1,0:T(8,128)(2,1)} %get-tuple-element.38), channel_id=1, source_target_pairs={{0,2},{2,0},{1,3},{3,1},{4,6},{6,4},{5,7},{7,5},{8,10},{10,8},{9,1... | collective-permute-start | bytes 2359304 | tf_op jit(solution)/shard_map/ppermute | solution.py:268
  56.3 0.9 copy-start.3
  59.6 36.5 %copy-start = (bf16[6144,128]{1,0:T(8,128)(2,1)S(1)}, bf16[6144,128]{1,0:T(8,128)(2,1)}, u32[]{:S(2)}) copy-start(bf16[6144,128]{1,0:T(8,128)(2,1)} %get-tuple-element.34.refs_0_.refs_4_) | copy-start | bytes 4718596
  59.6 36.5 %all-to-all-start.1 = ((bf16[4,6,240,128]{3,2,1,0:T(8,128)(2,1)}), bf16[4,6,240,128]{3,2,1,0:T(8,128)(2,1)}, u32[]{:S(2)}, u32[]{:S(2)}) async-start(bf16[4,6,240,128]{3,2,1,0:T(8,128)(2,1)} %broadcast_in_dim.67), calls=%async_computation.1 | async-start | bytes 2949120 | tf_op jit(solution)/shard_map/all_to_all | solution.py:281
  64.1 28.4 %collective-permute-start.7 = (bf16[128,3072]{1,0:T(8,128)(2,1)}, bf16[128,3072]{1,0:T(8,128)(2,1)}, u32[]{:S(2)}, u32[]{:S(2)}) collective-permute-start(bf16[128,3072]{1,0:T(8,128)(2,1)} %get-tuple-element.48), channel_id=1, source_target_pairs={{0,2},{2,0},{1,3},{3,1},{4,6},{6,4},{5,7},{7,5},{8,10},{10,8},{9,1... | collective-permute-start | bytes 2359304 | tf_op jit(solution)/shard_map/ppermute | solution.py:268
  75.7 20.4 %collective-permute-start.5 = (bf16[3072,128]{1,0:T(8,128)(2,1)}, bf16[3072,128]{1,0:T(8,128)(2,1)}, u32[]{:S(2)}, u32[]{:S(2)}) collective-permute-start(bf16[3072,128]{1,0:T(8,128)(2,1)} %collective-permute-done.2.refs_6_), channel_id=1, source_target_pairs={{0,1},{1,0},{2,3},{3,2},{4,5},{5,4},{6,7},{7,6},{8,9},{9,8},{10,11... | collective-permute-start | bytes 2359304 | tf_op jit(solution)/shard_map/ppermute | solution.py:274
  92.5 25.4 %collective-permute-start.8 = (bf16[128,3072]{1,0:T(8,128)(2,1)}, bf16[128,3072]{1,0:T(8,128)(2,1)}, u32[]{:S(2)}, u32[]{:S(2)}) collective-permute-start(bf16[128,3072]{1,0:T(8,128)(2,1)} %collective-permute-done.7.refs_2_), channel_id=1, source_target_pairs={{0,1},{1,0},{2,3},{3,2},{4,5},{5,4},{6,7},{7,6},{8,9},{9,8},{10,11... | collective-permute-start | bytes 2359304 | tf_op jit(solution)/shard_map/ppermute | solution.py:274
  96.1 21.8 %copy-start.2 = (bf16[128,3072]{1,0:T(8,128)(2,1)S(1)}, bf16[128,3072]{1,0:T(8,128)(2,1)}, u32[]{:S(2)}) copy-start(bf16[128,3072]{1,0:T(8,128)(2,1)} %get-tuple-element.35.refs_0_) | copy-start | bytes 2359300
  96.1 21.8 %copy-start.4 = (bf16[128,3072]{1,0:T(8,128)(2,1)S(1)}, bf16[128,3072]{1,0:T(8,128)(2,1)}, u32[]{:S(2)}) copy-start(bf16[128,3072]{1,0:T(8,128)(2,1)} %copy-done.3) | copy-start | bytes 2359300
  100.8 17.1 %collective-permute-start.6 = (bf16[240,1024]{1,0:T(8,128)(2,1)S(1)}, bf16[240,1024]{1,0:T(8,128)(2,1)S(1)}, u32[]{:S(2)}, u32[]{:S(2)}) collective-permute-start(bf16[240,1024]{1,0:T(8,128)(2,1)S(1)} %get-tuple-element.47), channel_id=1, source_target_pairs={{0,2},{2,0},{1,3},{3,1},{4,6},{6,4},{5,7},{7,5},{8,10},{10,8},{9,1... | collective-permute-start | bytes 1474568 | tf_op jit(solution)/shard_map/ppermute | solution.py:268
  103.2 7.5 %collective-permute-start.9 = (bf16[1,2,6,32,128]{4,3,2,1,0:T(8,128)(2,1)S(1)}, bf16[1,2,6,32,128]{4,3,2,1,0:T(8,128)(2,1)S(1)}, u32[]{:S(2)}, u32[]{:S(2)}) collective-permute-start(bf16[1,2,6,32,128]{4,3,2,1,0:T(8,128)(2,1)S(1)} %maximum_select_fusion), channel_id=1, source_target_pairs={{0,8},{4,12},{8,0},{12,4},{1,9},{5,13},{9,1},{13,5},{2,10},{6,14},... | collective-permute-start | bytes 294920 | tf_op jit(solution)/shard_map/ppermute | solution.py:271
  110.7 11.8 %copy-start.6 = (bf16[2,2,6,32,128]{4,3,2,1,0:T(8,128)(2,1)}, bf16[2,2,6,32,128]{4,3,2,1,0:T(8,128)(2,1)S(1)}, u32[]{:S(2)}) copy-start(bf16[2,2,6,32,128]{4,3,2,1,0:T(8,128)(2,1)S(1)} %pad_maximum_fusion.x_ref) | copy-start | bytes 589828
  110.7 7.2 %collective-permute-start.10 = (bf16[2,2,6,32,128]{4,3,2,1,0:T(8,128)(2,1)S(1)}, bf16[2,2,6,32,128]{4,3,2,1,0:T(8,128)(2,1)S(1)}, u32[]{:S(2)}, u32[]{:S(2)}) collective-permute-start(bf16[2,2,6,32,128]{4,3,2,1,0:T(8,128)(2,1)S(1)} %pad_maximum_fusion.x_ref), channel_id=1, source_target_pairs={{0,4},{4,0},{8,12},{12,8},{1,5},{5,1},{9,13},{13,9},{2,6},{6,2},{1... | collective-permute-start | bytes 589832 | tf_op jit(solution)/shard_map/ppermute | solution.py:271
  117.9 4.5 %copy-start.7 = (bf16[2,2,6,32,128]{4,3,2,1,0:T(8,128)(2,1)}, bf16[2,2,6,32,128]{4,3,2,1,0:T(8,128)(2,1)S(1)}, u32[]{:S(2)}) copy-start(bf16[2,2,6,32,128]{4,3,2,1,0:T(8,128)(2,1)S(1)} %collective-permute-done.10.r_ref) | copy-start | bytes 589828
  122.4 3.6 %copy-start.9 = (s32[4]{0:T(128)S(1)}, s32[4]{0:T(128)}, u32[]{:S(2)}) copy-start(s32[4]{0:T(128)} %constant.63.clone) | copy-start | bytes 52
  122.5 21.3 %all-to-all-start.2 = ((bf16[4,6,240,128]{3,2,1,0:T(8,128)(2,1)}), bf16[4,6,240,128]{3,2,1,0:T(8,128)(2,1)S(1)}, u32[]{:S(2)}, u32[]{:S(2)}) async-start(bf16[4,6,240,128]{3,2,1,0:T(8,128)(2,1)} %down.1), calls=%async_computation.2 | async-start | bytes 2949120 | tf_op jit(solution)/shard_map/all_to_all | solution.py:281
  134.6 24.1 %collective-permute-start.11 = (bf16[2,2,6,32,128]{4,3,2,1,0:T(8,128)(2,1)S(1)}, bf16[2,2,6,32,128]{4,3,2,1,0:T(8,128)(2,1)S(1)}, u32[]{:S(2)}, u32[]{:S(2)}) collective-permute-start(bf16[2,2,6,32,128]{4,3,2,1,0:T(8,128)(2,1)S(1)} %slice.50), channel_id=1, source_target_pairs={{0,4},{4,0},{8,12},{12,8},{1,5},{5,1},{9,13},{13,9},{2,6},{6,2},{1... | collective-permute-start | bytes 589832 | tf_op jit(solution)/shard_map/ppermute | solution.py:271
  144.0 14.7 %copy-start.5 = (bf16[4,2,6,32,128]{4,3,2,1,0:T(8,128)(2,1)S(1)}, bf16[4,2,6,32,128]{4,3,2,1,0:T(8,128)(2,1)}, u32[]{:S(2)}) copy-start(bf16[4,2,6,32,128]{4,3,2,1,0:T(8,128)(2,1)} %shared.1) | copy-start | bytes 1179652
  144.9 31.8 %all-to-all-start.3 = ((bf16[48,32,128]{2,1,0:T(8,128)(2,1)}), bf16[48,32,128]{2,1,0:T(8,128)(2,1)S(1)}, u32[]{:S(2)}, u32[]{:S(2)}) async-start(bf16[48,32,128]{2,1,0:T(8,128)(2,1)} %copy.33), calls=%async_computation.3 | async-start | bytes 786432 | tf_op jit(solution)/shard_map/all_to_all | solution.py:281
  158.8 6.9 %collective-permute-start.12 = (bf16[1,2,6,32,128]{4,3,2,1,0:T(8,128)(2,1)S(1)}, bf16[1,2,6,32,128]{4,3,2,1,0:T(8,128)(2,1)S(1)}, u32[]{:S(2)}, u32[]{:S(2)}) collective-permute-start(bf16[1,2,6,32,128]{4,3,2,1,0:T(8,128)(2,1)S(1)} %slice.52), channel_id=1, source_target_pairs={{0,8},{4,12},{8,0},{12,4},{1,9},{5,13},{9,1},{13,5},{2,10},{6,14},... | collective-permute-start | bytes 294920 | tf_op jit(solution)/shard_map/ppermute | solution.py:271
  165.8 6.1 %collective-permute-start.13 = (bf16[6,32,128]{2,1,0:T(8,128)(2,1)S(1)}, bf16[6,32,128]{2,1,0:T(8,128)(2,1)S(1)}, u32[]{:S(2)}, u32[]{:S(2)}) collective-permute-start(bf16[6,32,128]{2,1,0:T(8,128)(2,1)S(1)} %select_bitcast_fusion), channel_id=1, source_target_pairs={{0,2},{2,0},{1,3},{3,1},{4,6},{6,4},{5,7},{7,5},{8,10},{10,8},{9,1... | collective-permute-start | bytes 147464 | tf_op jit(solution)/shard_map/ppermute | solution.py:268
  177.4 10.9 %collective-permute-start.14 = (f32[3,32,128]{2,1,0:T(8,128)S(1)}, f32[3,32,128]{2,1,0:T(8,128)S(1)}, u32[]{:S(2)}, u32[]{:S(2)}) collective-permute-start(f32[3,32,128]{2,1,0:T(8,128)S(1)} %slice_select_fusion), channel_id=1, source_target_pairs={{0,1},{1,0},{2,3},{3,2},{4,5},{5,4},{6,7},{7,6},{8,9},{9,8},{10,11... | collective-permute-start | bytes 147464 | tf_op jit(solution)/shard_map/ppermute | solution.py:359
